TPU v7x, 32 devices: a whole 2x2x4 slice. The times are simulated.
32 devices in a mesh: gx: 4 (over z), gy: 4 (over y, core), gz: 2 (over x).
Axes of the slice: x: 2, y: 2, z: 4, core: 2. Of those that a mesh axis runs over, the one named last changes fastest.
Arguments:
- right_side: float32 [128, 128, 256], P('gx', 'gy', 'gz'), may hold values from -8 to 8
- guess: float32 [128, 128, 256], P('gx', 'gy', 'gz'), may hold values from -4 to 4
Outputs:
- solution_field: float32 [128, 128, 256], P('gx', 'gy', 'gz')
- residual: float32 [128, 128, 256], P('gx', 'gy', 'gz')
All inputs are finite; a program needn't handle non-finite values.
Results may differ from a plain program's by a relative error of at most 0.0001.
Values sent between devices are 32-bit elements; how exact they have to be, the bound alone decides.
A program may use at most 128 MiB of HBM per device.

v0:
```python
import functools

import jax
import jax.numpy as jnp
from jax import lax
from jax.experimental import pallas as pl
from jax.experimental.pallas import tpu as pltpu
from jax.sharding import PartitionSpec as P

LEVELS = 6
SWEEPS = 4
STEPS = 2
HALOED = 3
AXES = ("gx", "gy", "gz")
LANES = 128
TOP = 8
MESH = pl.DeviceIdType.MESH
ROUNDS = 1 + STEPS * SWEEPS
HIGH = lax.Precision.HIGHEST


def iota(shape, dim):
    return lax.broadcasted_iota(jnp.int32, shape, dim)


def lanes_dot(x, matrix):
    first, second, _ = x.shape
    if second % 8 == 0:
        out = jnp.dot(x.reshape(first * second, LANES), matrix, precision=HIGH, preferred_element_type=jnp.float32)
        return out.reshape(first, second, LANES)
    planes = [jnp.dot(x[i], matrix, precision=HIGH, preferred_element_type=jnp.float32)[None] for i in range(first)]
    return jnp.concatenate(planes, axis=0)


def halve_matrix(width, start):
    source, target = iota((LANES, LANES), 0), iota((LANES, LANES), 1) - start
    keep = (target >= 0) & (target < width) & ((source == 2 * target) | (source == 2 * target + 1))
    return jnp.where(keep, 0.125, 0.0)


def double_matrix(width, start):
    source, target = iota((LANES, LANES), 0) - start, iota((LANES, LANES), 1)
    keep = (source >= 0) & (source < width) & ((target == 2 * source) | (target == 2 * source + 1))
    return jnp.where(keep, 1.0, 0.0)


def plane_groups(shape, width):
    return max(1, LANES // width // shape[1])


def own_group(shape, width):
    group = iota(shape, 0) % plane_groups(shape, width) * shape[1] + iota(shape, 1)
    return iota(shape, 2) // width == group


def tile_matrix(width):
    source, target = iota((LANES, LANES), 0), iota((LANES, LANES), 1) % width
    return jnp.where((source == 2 * target) | (source == 2 * target + 1), 0.125, 0.0)


def gather_matrix(width, start):
    source, target = iota((LANES, LANES), 0) % width, iota((LANES, LANES), 1) - start
    return jnp.where(source == target, 1.0, 0.0)


def kernel(sizes, block, b_ref, x_ref, sol_ref, res_ref, *rest):
    (u0a, u0b, u1a, u1b, u2a, u2b, g0, g1, g2, wref, fold, spread,
     xs, xr, ys, yr, zs, zr, gs, gr, ds, dr,
     hsend, hrecv, gsend, grecv, dsend, drecv) = rest
    us = ((u0a, u0b), (u1a, u1b), (u2a, u2b))
    gref = (g0, g1, g2)
    nx, ny, nz = sizes
    n = nx * ny * nz
    at = tuple(lax.axis_index(a) for a in AXES)
    me = (at[0] * ny + at[1]) * nz + at[2]
    dims = [tuple(d >> l for d in block) for l in range(LEVELS)]

    def others():
        moved = [[lax.rem(at[d] + k, sizes[d]) if k else at[d] for k in range(sizes[d])] for d in range(3)]
        return [(a, b, c) for a in moved[0] for b in moved[1] for c in moved[2]][1:]

    xr[...] = jnp.zeros_like(xr)
    yr[...] = jnp.zeros_like(yr)
    zr[...] = jnp.zeros_like(zr)

    barrier = pltpu.get_barrier_semaphore()

    for target in others():
        pl.semaphore_signal(barrier, inc=1, device_id=target, device_id_type=MESH)

    row_off, lane_off = [0], [0]
    for l in range(HALOED):
        row_off.append(row_off[-1] + dims[l][0])
        lane_off.append(lane_off[-1] + 2 * dims[l][0])

    def halo_copies(r, levels):
        rows = row_off[levels]
        out = []
        for d, (s, t) in enumerate(((xs, xr), (ys, yr), (zs, zr))):
            for side in (0, 1):
                target = list(at)
                target[d] = at[d] + (1 if side else -1)
                src = s.at[r] if d == 2 else s.at[r, side, pl.ds(0, rows)]
                dst = t.at[r, side] if d == 2 else t.at[r, side, pl.ds(0, rows)]
                copy = pltpu.make_async_remote_copy(
                    src_ref=src, dst_ref=dst,
                    send_sem=hsend.at[r, 2 * d + side], recv_sem=hrecv.at[r, 2 * d + side],
                    device_id=tuple(target), device_id_type=MESH,
                )
                lower, upper = at[d] > 0, at[d] < sizes[d] - 1
                out.append((copy, upper if side else lower, lower if side else upper))
        return out

    def send(r, fields, levels, before=lambda: None):
        for l in range(levels):
            X, Y, Z = dims[l]
            u = fields[l]
            o = row_off[l]
            for side, i in ((0, 1), (1, X)):
                xs[r, side, o:o + Y, :] = u[i, TOP:TOP + Y, :]
            for side, j in ((0, TOP), (1, TOP + Y - 1)):
                ys[r, side, o:o + X, :, :] = u[1:X + 1, j:j + 1, :]
            body = u[1:X + 1, TOP:TOP + Y, :]
            lane, plane = iota((X, Y, LANES), 2) - lane_off[l], iota((X, Y, LANES), 0)
            packed = jnp.where(lane == plane, body[:, :, Z - 1:Z], jnp.where(lane == plane + X, body[:, :, 0:1], 0.0))
            packed = jnp.sum(packed, axis=0)
            zs[r, 0:Y, :] = packed if l == 0 else zs[r, 0:Y, :] + packed
        before()
        for copy, cond, _ in halo_copies(r, levels):
            pl.when(cond)(copy.start)

    def receive(r, fields, levels):
        for copy, _, cond in halo_copies(r, levels):
            pl.when(cond)(copy.wait_recv)
        for l in range(levels):
            X, Y, Z = dims[l]
            u = fields[l]
            o = row_off[l]
            u[0, TOP:TOP + Y, :] = xr[r, 1, o:o + Y, :]
            u[X + 1, TOP:TOP + Y, :] = xr[r, 0, o:o + Y, :]
            u[1:X + 1, TOP - 1:TOP, :] = yr[r, 1, o:o + X, :, :]
            u[1:X + 1, TOP + Y:TOP + Y + 1, :] = yr[r, 0, o:o + X, :, :]

    def beside(r, u, l, x0, c):
        X, Y, Z = dims[l]
        mid = u[x0 + 1:x0 + 1 + c, TOP:TOP + Y, :]
        total = u[x0:x0 + c, TOP:TOP + Y, :] + u[x0 + 2:x0 + 2 + c, TOP:TOP + Y, :]
        total = total + u[x0 + 1:x0 + 1 + c, TOP - 1:TOP - 1 + Y, :]
        total = total + u[x0 + 1:x0 + 1 + c, TOP + 1:TOP + 1 + Y, :]
        lane = iota((c, Y, LANES), 2)
        o = lane_off[l] + x0
        low, high = zr[r, 1, 0:Y, :], zr[r, 0, 0:Y, :]
        below = jnp.concatenate([low[:, o + i:o + i + 1][None] for i in range(c)], axis=0)
        above = jnp.concatenate([high[:, o + X + i:o + X + i + 1][None] for i in range(c)], axis=0)
        total = total + jnp.where(lane == 0, below, pltpu.roll(mid, 1, 2))
        total = total + jnp.where(lane == Z - 1, above, pltpu.roll(mid, LANES - 1, 2))
        return mid, total

    def chunks(l):
        c = min(dims[l][0], 8)
        return [(x0, c) for x0 in range(0, dims[l][0], c)]

    def inside(l, x0, c):
        return (slice(x0 + 1, x0 + 1 + c), slice(TOP, TOP + dims[l][1]), slice(None))

    def fold_xy(field):
        X, Y, _ = field.shape
        pairs = field.reshape(X // 2, 2, Y, LANES)
        fold[0:X // 2, 0:Y, :] = pairs[:, 0] + pairs[:, 1]
        return fold[0:X // 2, pl.ds(0, Y // 2, 2), :] + fold[0:X // 2, pl.ds(1, Y // 2, 2), :]

    def spread_y(field):
        X, Y, _ = field.shape
        spread[0:X, pl.ds(0, Y, 2), :] = field
        spread[0:X, pl.ds(1, Y, 2), :] = field

    def twice(field):
        X, Y, _ = field.shape
        return jnp.broadcast_to(field[:, None], (X, 2, Y, LANES)).reshape(2 * X, Y, LANES)

    def to_all(step, src, dst, s_sem, r_sem):
        for target in others():
            pltpu.make_async_remote_copy(
                src_ref=src.at[step], dst_ref=dst.at[step, me], send_sem=s_sem.at[step], recv_sem=r_sem.at[step],
                device_id=target, device_id_type=MESH,
            ).start()

    def all_done(step, dst, sem):
        part = dst.at[step, pl.ds(0, n - 1)]
        pltpu.make_async_copy(part, part, sem.at[step]).wait()

    X, Y, Z = dims[0]
    u0a[1:X + 1, TOP:TOP + Y, :] = x_ref[...]
    sol_ref[...] = x_ref[...]
    send(0, [u0a], 1, lambda: pl.semaphore_wait(barrier, n - 1))
    receive(0, [u0a], 1)
    for x0, c in chunks(0):
        mid, total = beside(0, u0a, 0, x0, c)
        g0[x0:x0 + c] = b_ref[x0:x0 + c] - (6.0 * mid - total)

    def smooth_whole(rhs, width, l):
        X, Y, _ = rhs.shape
        lane = iota(rhs.shape, 2)
        e = rhs
        for _ in range(SWEEPS - 1):
            px, py = jnp.zeros((1, Y, LANES), jnp.float32), jnp.zeros((X, 1, LANES), jnp.float32)
            total = jnp.concatenate([px, e[:-1]], axis=0) + jnp.concatenate([e[1:], px], axis=0)
            total = total + jnp.concatenate([py, e[:, :-1]], axis=1) + jnp.concatenate([e[:, 1:], py], axis=1)
            total = total + jnp.where(lane == 0, 0.0, pltpu.roll(e, 1, 2))
            total = total + jnp.where(lane == width - 1, 0.0, pltpu.roll(e, LANES - 1, 2))
            e = rhs + (3.0 * e + total) * (1.0 / 9.0)
        return e * (4.0 ** l / 9.0)

    for step in range(STEPS):
        base = 1 + step * SWEEPS
        for l in range(HALOED - 1):
            gref[l + 1][...] = lanes_dot(fold_xy(gref[l][...]), halve_matrix(dims[l + 1][2], 0))
        width = dims[HALOED][2]
        own = lanes_dot(fold_xy(gref[HALOED - 1][...]), tile_matrix(width))
        own = jnp.where(own_group(own.shape, width), own, 0.0)
        own = jnp.sum(own.reshape(-1, plane_groups(own.shape, width), *own.shape[1:]), axis=1)
        own = jnp.sum(own, axis=1, keepdims=True)
        gs[step] = own
        gr[step, me] = own
        to_all(step, gs, gr, gsend, grecv)
        for l in range(HALOED):
            us[l][0][1:dims[l][0] + 1, TOP:TOP + dims[l][1], :] = gref[l][...]
        for sweep in range(SWEEPS - 1):
            r = base + sweep
            fields = [us[l][sweep % 2] for l in range(HALOED)]
            later = [us[l][(sweep + 1) % 2] for l in range(HALOED)]
            send(r, fields, HALOED)
            if sweep == SWEEPS - 2:
                all_done(step, gr, grecv)
                cx, cy, _ = dims[HALOED]
                per = plane_groups((cx, cy), width)
                fine = None
                for k in range(nz):
                    rows = []
                    for i in range(nx):
                        columns = []
                        for j in range(ny):
                            part = gr[step, (i * ny + j) * nz + k][:, None]
                            part = jnp.broadcast_to(part, (cx // per, per, cy, LANES)).reshape(cx, cy, LANES)
                            columns.append(jnp.where(own_group((cx, cy, LANES), width), part, 0.0))
                        rows.append(jnp.concatenate(columns, axis=1))
                    spot = lanes_dot(jnp.concatenate(rows, axis=0), gather_matrix(width, k * width))
                    fine = spot if fine is None else fine + spot
                chain = [fine]
                widths = [width * nz]
                for l in range(HALOED + 1, LEVELS):
                    widths.append(widths[-1] // 2)
                    chain.append(lanes_dot(fold_xy(chain[-1]), halve_matrix(widths[-1], 0)))
                whole = smooth_whole(chain[-1], widths[-1], LEVELS - 1)
                for l in range(LEVELS - 2, HALOED - 1, -1):
                    i = l - HALOED
                    spread_y(whole)
                    grown = spread[0:whole.shape[0], 0:2 * whole.shape[1], :]
                    grown = twice(lanes_dot(grown, double_matrix(widths[i + 1], 0)))
                    whole = grown + smooth_whole(chain[i], widths[i], l)
                wref[...] = whole
            receive(r, fields, HALOED)
            for l in range(HALOED):
                for x0, c in chunks(l):
                    mid, total = beside(r, fields[l], l, x0, c)
                    later[l][inside(l, x0, c)] = gref[l][x0:x0 + c] + (3.0 * mid + total) * (1.0 / 9.0)
        ends = [us[l][(SWEEPS - 1) % 2] for l in range(HALOED)]
        cx, cy, _ = dims[HALOED]
        spread_y(wref[pl.ds(at[0] * cx, cx)])
        part = spread[0:cx, pl.ds(pl.multiple_of(at[1] * 2 * cy, 8), 2 * cy), :]
        part = lanes_dot(part, double_matrix(width, at[2] * width))
        for l in range(HALOED - 1, -1, -1):
            X, Y, Z = dims[l]
            full = ends[l][1:X + 1, TOP:TOP + Y, :] * (4.0 ** l / 9.0) + twice(part)
            if l:
                spread_y(full)
                part = lanes_dot(spread[0:X, 0:2 * Y, :], double_matrix(Z, 0))
            else:
                ends[0][1:X + 1, TOP:TOP + Y, :] = full
        r = base + SWEEPS - 1
        z = ends[0]
        w = us[0][SWEEPS % 2]
        send(r, [z], 1)
        receive(r, [z], 1)
        rz = jnp.zeros((Y, LANES), jnp.float32)
        zw = jnp.zeros((Y, LANES), jnp.float32)
        for x0, c in chunks(0):
            mid, total = beside(r, z, 0, x0, c)
            image = 6.0 * mid - total
            w[inside(0, x0, c)] = image
            rz = rz + jnp.sum(g0[x0:x0 + c] * mid, axis=0)
            zw = zw + jnp.sum(mid * image, axis=0)
        sums = jnp.concatenate([jnp.sum(rz, axis=0, keepdims=True), jnp.sum(zw, axis=0, keepdims=True)], axis=0)
        ds[step] = sums
        dr[step, me] = sums
        to_all(step, ds, dr, dsend, drecv)
        all_done(step, dr, drecv)
        both = jnp.sum(dr[step], axis=0)
        both = jnp.sum(both, axis=1, keepdims=True)
        alpha = (both[0:1] / both[1:2])[None]
        for x0, c in chunks(0):
            sol_ref[x0:x0 + c] = sol_ref[x0:x0 + c] + alpha * z[inside(0, x0, c)]
            renewed = g0[x0:x0 + c] - alpha * w[inside(0, x0, c)]
            if step == STEPS - 1:
                res_ref[x0:x0 + c] = renewed
            else:
                g0[x0:x0 + c] = renewed

    for step in range(STEPS):
        all_done(step, gr, gsend)
        all_done(step, dr, dsend)
    for r in range(ROUNDS):
        for copy, cond, _ in halo_copies(r, 1 if r % SWEEPS == 0 else HALOED):
            pl.when(cond)(copy.wait_send)


def solution(mesh):
    sizes = tuple(mesh.shape[a] for a in AXES)
    n = sizes[0] * sizes[1] * sizes[2]

    def run(right_side, guess):
        X, Y, Z = block = guess.shape
        dims = [tuple(d >> l for d in block) for l in range(LEVELS)]
        rows = sum(dims[l][0] for l in range(HALOED))
        f32 = jnp.float32
        vm = lambda *s: pltpu.VMEM(s, f32)
        padded = [vm(dims[l][0] + 2, dims[l][1] + 2 * TOP, LANES) for l in range(HALOED) for _ in range(2)]
        cx, cy, width = dims[HALOED]
        packed = cx // plane_groups((cx, cy), width)
        scratch = padded + [vm(dims[l][0], dims[l][1], LANES) for l in range(HALOED)] + [
            vm(cx * sizes[0], cy * sizes[1], LANES),
            vm(X // 2, Y, LANES), vm(X // 2, Y, LANES),
            vm(ROUNDS, 2, rows, LANES), vm(ROUNDS, 2, rows, LANES),
            vm(ROUNDS, 2, rows, 1, LANES), vm(ROUNDS, 2, rows, 1, LANES),
            vm(ROUNDS, Y, LANES), vm(ROUNDS, 2, Y, LANES),
            vm(STEPS, packed, 1, LANES), vm(STEPS, n, packed, 1, LANES),
            vm(STEPS, 2, LANES), vm(STEPS, n, 2, LANES),
            pltpu.SemaphoreType.DMA((ROUNDS, 6)), pltpu.SemaphoreType.DMA((ROUNDS, 6)),
        ] + [pltpu.SemaphoreType.DMA((STEPS,))] * 4
        out = jax.ShapeDtypeStruct(block, f32)
        return tuple(pl.pallas_call(
            functools.partial(kernel, sizes, block),
            out_shape=(out, out),
            in_specs=[pl.BlockSpec(memory_space=pltpu.VMEM)] * 2,
            out_specs=[pl.BlockSpec(memory_space=pltpu.VMEM)] * 2,
            scratch_shapes=scratch,
            compiler_params=pltpu.CompilerParams(collective_id=0, has_side_effects=True),
        )(right_side, guess))

    spec = P(*AXES)
    return jax.shard_map(run, mesh=mesh, in_specs=(spec, spec), out_specs=(spec, spec), check_vma=False)
```

profile of v0, /device:TPU:0, one launch (start us, length us, event | category | flops | bytes accessed | tf_op | source)
XLA Modules:
  0.0 65.6 jit_solution(8860012439118518115)
XLA Ops:
  0.6 62.2 %shard_map.41 = (f32[32,32,128]{2,1,0:T(8,128)}, f32[32,32,128]{2,1,0:T(8,128)}) custom-call(f32[32,32,128]{2,1,0:T(8,128)} %b_ref.1, f32[32,32,128]{2,1,0:T(8,128)} %x_ref.1), custom_call_target="tpu_custom_call" | custom-call | tf_op jit(solution)/shard_map/pallas_call | solution.py:341
  62.9 0.0 copy-start
  62.9 1.9 %copy.6 = f32[32,32,128]{2,1,0:T(8,128)} copy(f32[32,32,128]{2,1,0:T(8,128)} %get-tuple-element.4) | data formatting | bytes 1048576
  64.8 0.0 copy-done
  64.8 0.8 %copy.7 = f32[32,32,128]{2,1,0:T(8,128)} copy(f32[32,32,128]{2,1,0:T(8,128)S(1)} %copy-done) | data formatting | bytes 1048576
Async XLA Ops:
  62.9 1.9 %copy-start = (f32[32,32,128]{2,1,0:T(8,128)S(1)}, f32[32,32,128]{2,1,0:T(8,128)}, u32[]{:S(2)}) copy-start(f32[32,32,128]{2,1,0:T(8,128)} %get-tuple-element.5) | copy-start | bytes 1572868
where the time goes:
time: 65.8 us; the launch traced here: 65.6 us
  Pallas kernels  62.2 us (95%)
  local copies, waits for them, and re-layouts  2.72 us (4%)
    pallas_call x1, Pallas kernels, run(): pl.pallas_call(functools.partial(kernel, sizes, block), out_shape=(out, o...  62.2 us
    unnamed x4, local copies, waits for them, and re-layouts  2.72 us

commit v1 on v0

v1 whole, which is shorter than its diff:
```python
import functools

import jax
import jax.numpy as jnp
from jax import lax
from jax.experimental import pallas as pl
from jax.experimental.pallas import tpu as pltpu
from jax.sharding import PartitionSpec as P

LEVELS = 6
SWEEPS = 4
STEPS = 2
HALOED = 3
AXES = ("gx", "gy", "gz")
LANES = 128
TOP = 8
DEPTH = SWEEPS
SPAN = 8 * DEPTH
PER = LANES // SPAN
MESH = pl.DeviceIdType.MESH
HIGH = lax.Precision.HIGHEST
AROUND = [(a, b) for a in (-1, 0, 1) for b in (-1, 0, 1) if (a, b) != (0, 0)]
FACES = [(d, s) for d in range(3) for s in (-1, 1)]


def iota(shape, dim):
    return lax.broadcasted_iota(jnp.int32, shape, dim)


def lanes_dot(x, matrix):
    first, second, _ = x.shape
    if second % 8 == 0:
        out = jnp.dot(x.reshape(first * second, LANES), matrix, precision=HIGH, preferred_element_type=jnp.float32)
        return out.reshape(first, second, LANES)
    planes = [jnp.dot(x[i], matrix, precision=HIGH, preferred_element_type=jnp.float32)[None] for i in range(first)]
    return jnp.concatenate(planes, axis=0)


def halve_matrix(width, start):
    source, target = iota((LANES, LANES), 0), iota((LANES, LANES), 1) - start
    keep = (target >= 0) & (target < width) & ((source == 2 * target) | (source == 2 * target + 1))
    return jnp.where(keep, 0.125, 0.0)


def double_matrix(width, start):
    source, target = iota((LANES, LANES), 0) - start, iota((LANES, LANES), 1)
    keep = (source >= 0) & (source < width) & ((target == 2 * source) | (target == 2 * source + 1))
    return jnp.where(keep, 1.0, 0.0)


def wrapped(lane):
    return jnp.where(lane >= LANES - DEPTH, lane - LANES, lane)


def double_around(coarse_start, coarse_total, fine_width):
    source, target = iota((LANES, LANES), 0), wrapped(iota((LANES, LANES), 1))
    at = (target >> 1) + coarse_start
    if coarse_total is None:
        at = at & (LANES - 1)
        keep = (source == at) & (target < fine_width + DEPTH)
    else:
        keep = (source == at) & (target < fine_width + DEPTH) & (source < coarse_total)
    return jnp.where(keep, 1.0, 0.0)


def ends_matrix(width):
    source, target = iota((LANES, LANES), 0), iota((LANES, LANES), 1)
    keep = ((target == 0) & (source == LANES - 1)) | ((target == LANES - 1) & (source == width))
    return jnp.where(keep, 1.0, 0.0)


def plane_groups(shape, width):
    return max(1, LANES // width // shape[1])


def own_group(shape, width):
    group = iota(shape, 0) % plane_groups(shape, width) * shape[1] + iota(shape, 1)
    return iota(shape, 2) // width == group


def tile_matrix(width):
    source, target = iota((LANES, LANES), 0), iota((LANES, LANES), 1) % width
    return jnp.where((source == 2 * target) | (source == 2 * target + 1), 0.125, 0.0)


def gather_matrix(width, start):
    source, target = iota((LANES, LANES), 0) % width, iota((LANES, LANES), 1) - start
    return jnp.where(source == target, 1.0, 0.0)


def turn(x, shift):
    shift = shift % LANES
    return pltpu.roll(x, shift, x.ndim - 1) if shift else x


def kernel(sizes, block, b_hbm, x_hbm, sol_ref, res_ref, *rest):
    (ux, bb, g0, g1, g2, gs, f0a, f0b, f1a, f1b, f2a, f2b, fsa, fsb, z0, z1, wv, sc, sd, pd, pe,
     m0, m1, m2, ms, wref, wide, fold, spread, ze, zi, zs, zr, cs, cr, ds, dr,
     isem, xsend, xrecv, zsend, zrecv, msend, mrecv, fsend, frecv, csend, crecv, dsend, drecv) = rest
    nx, ny, nz = sizes
    n = nx * ny * nz
    at = tuple(lax.axis_index(a) for a in AXES)
    me = (at[0] * ny + at[1]) * nz + at[2]
    dims = [tuple(d >> l for d in block) for l in range(LEVELS)]
    X, Y, Z = block
    fields = (g0, g1, g2)
    ping = ((f0a, f0b), (f1a, f1b), (f2a, f2b))
    masks = (m0, m1, m2)
    groups = X // PER
    lower = [at[d] > 0 for d in range(3)]
    upper = [at[d] < sizes[d] - 1 for d in range(3)]
    inlow = [jnp.where(c, 1.0, 0.0) for c in lower]
    inup = [jnp.where(c, 1.0, 0.0) for c in upper]

    load_x = pltpu.make_async_copy(x_hbm, ux.at[1:X + 1, TOP:TOP + Y], isem.at[0])
    load_b = pltpu.make_async_copy(b_hbm, bb, isem.at[1])
    load_x.start()
    load_b.start()

    def others():
        moved = [[lax.rem(at[d] + k, sizes[d]) if k else at[d] for k in range(sizes[d])] for d in range(3)]
        return [(a, b, c) for a in moved[0] for b in moved[1] for c in moved[2]][1:]

    def clear(ref, lead, planes, depth, rows, own):
        zero = jnp.float32(0)
        for i in lead:
            head = (i,) if i is not None else ()
            for a, b in ((0, depth), (planes - depth, planes)):
                ref[head + (slice(a, b),)] = jnp.full((b - a,) + ref.shape[-2:], zero)
            for a, b in ((0, TOP), (TOP + own, rows)):
                ref[head + (slice(depth, planes - depth), slice(a, b))] = jnp.full((planes - 2 * depth, b - a, LANES), zero)

    clear(ux, (None,), X + 2, 1, Y + 2 * TOP, Y)
    for l in range(HALOED):
        clear(fields[l], range(STEPS), dims[l][0] + 2 * DEPTH, DEPTH, dims[l][1] + 2 * TOP, dims[l][1])
    clear(gs, range(STEPS), groups + 2, 1, Y + 2 * TOP, Y)
    zi[...] = jnp.zeros_like(zi)
    zr[...] = jnp.zeros_like(zr)

    barrier = pltpu.get_barrier_semaphore()
    for target in others():
        pl.semaphore_signal(barrier, inc=1, device_id=target, device_id_type=MESH)

    for ref in (f0a, f0b, f1a, f1b, f2a, f2b, fsa, fsb):
        ref[...] = jnp.zeros_like(ref)
    wref[...] = jnp.zeros_like(wref)
    wide[...] = jnp.zeros_like(wide)

    def mask(rows, z, depth_z):
        y = iota((rows + 2 * DEPTH, LANES), 0) - DEPTH
        part = jnp.where(y < 0, inlow[1], jnp.where(y >= rows, inup[1], 1.0))
        return part * jnp.where(z < 0, inlow[2], jnp.where(z >= depth_z, inup[2], 1.0)) * (1.0 / 9.0)

    for l in range(HALOED):
        lane = iota((dims[l][1] + 2 * DEPTH, LANES), 1)
        masks[l][...] = mask(dims[l][1], lane if l == 0 else wrapped(lane), dims[l][2])
    lane = iota((Y + 2 * DEPTH, LANES), 1) % SPAN
    ms[...] = mask(Y, jnp.where(lane < SPAN // 2, lane + Z - SPAN // 4, lane - 3 * SPAN // 4), Z)

    def face_copies():
        out = []
        for i, (d, s) in enumerate(FACES):
            target = list(at)
            target[d] = at[d] + s
            if d == 0:
                src, dst = (X, 0) if s > 0 else (1, X + 1)
                src, dst = ux.at[src:src + 1, TOP:TOP + Y], ux.at[dst:dst + 1, TOP:TOP + Y]
            elif d == 1:
                src, dst = (TOP + Y - 1, TOP - 1) if s > 0 else (TOP, TOP + Y)
                src, dst = ux.at[1:X + 1, src:src + 1], ux.at[1:X + 1, dst:dst + 1]
            else:
                src, dst = ze, zi.at[0 if s > 0 else 1]
            copy = pltpu.make_async_remote_copy(
                src_ref=src, dst_ref=dst, send_sem=xsend.at[i], recv_sem=xrecv.at[i],
                device_id=tuple(target), device_id_type=MESH,
            )
            out.append((copy, upper[d] if s > 0 else lower[d], lower[d] if s > 0 else upper[d]))
        return out

    def z_copies(k):
        out = []
        for side in (0, 1):
            copy = pltpu.make_async_remote_copy(
                src_ref=zs.at[k, side], dst_ref=zr.at[k, side], send_sem=zsend.at[k, side], recv_sem=zrecv.at[k, side],
                device_id=(at[0], at[1], at[2] + (1 if side else -1)), device_id_type=MESH,
            )
            out.append((copy, upper[2] if side else lower[2], lower[2] if side else upper[2]))
        return out

    def span(step, depth, start, own, other):
        if step > 0:
            return (start + own - depth, depth), (start - depth, depth)
        if step < 0:
            return (start, depth), (start + own, depth)
        return (start, own), (start, own)

    def around_copies(ref, k, depth, planes, rows, ssem, rsem):
        out = []
        for i, (dx, dy) in enumerate(AROUND):
            (sx, lx), (tx, _) = span(dx, depth, depth, planes, None)
            (sy, ly), (ty, _) = span(dy, DEPTH, TOP, rows, None)
            copy = pltpu.make_async_remote_copy(
                src_ref=ref.at[k, sx:sx + lx, sy:sy + ly], dst_ref=ref.at[k, tx:tx + lx, ty:ty + ly],
                send_sem=ssem(i), recv_sem=rsem(i),
                device_id=(at[0] + dx, at[1] + dy, at[2]), device_id_type=MESH,
            )
            to, fro = None, None
            for d, s in ((0, dx), (1, dy)):
                if s:
                    a, b = (upper[d], lower[d]) if s > 0 else (lower[d], upper[d])
                    to = a if to is None else jnp.logical_and(to, a)
                    fro = b if fro is None else jnp.logical_and(fro, b)
            out.append((copy, to, fro))
        return out

    def main_copies(k):
        return around_copies(g0, k, DEPTH, X, Y, lambda i: msend.at[k, i], lambda i: mrecv.at[k, i])

    def more_copies(k):
        out = [around_copies(gs, k, 1, groups, Y, lambda i: fsend.at[k, 0, i], lambda i: frecv.at[k, 0, i])]
        for l in range(1, HALOED):
            out.append(around_copies(
                fields[l], k, DEPTH, dims[l][0], dims[l][1],
                lambda i, l=l: fsend.at[k, l, i], lambda i, l=l: frecv.at[k, l, i]))
        return [[kind[i] for kind in out] for i in range(len(AROUND))]

    def start_all(copies):
        for copy, cond, _ in copies:
            pl.when(cond)(copy.start)

    def wait_all(copies):
        for copy, _, cond in copies:
            pl.when(cond)(copy.wait_recv)

    def sent_all(copies):
        for copy, cond, _ in copies:
            pl.when(cond)(copy.wait_send)

    def start_more(k):
        for same in more_copies(k):
            @pl.when(same[0][1])
            def _(same=same):
                for copy, _, _ in same:
                    copy.start()

    def wait_more(k):
        for same in more_copies(k):
            @pl.when(same[0][2])
            def _(same=same):
                for copy, _, _ in same:
                    copy.wait_recv()

    def sent_more(k):
        for same in more_copies(k):
            @pl.when(same[0][1])
            def _(same=same):
                for copy, _, _ in same:
                    copy.wait_send()

    def to_all(src, dst, s_sem, r_sem):
        for target in others():
            pltpu.make_async_remote_copy(
                src_ref=src, dst_ref=dst.at[me], send_sem=s_sem, recv_sem=r_sem,
                device_id=target, device_id_type=MESH,
            ).start()

    def all_done(dst, sem):
        part = dst.at[pl.ds(0, n - 1)]
        pltpu.make_async_copy(part, part, sem).wait()

    def fold_xy(field):
        A, B, _ = field.shape
        pairs = field.reshape(A // 2, 2, B, LANES)
        fold[0:A // 2, 0:B, :] = pairs[:, 0] + pairs[:, 1]
        return fold[0:A // 2, pl.ds(0, B // 2, 2), :] + fold[0:A // 2, pl.ds(1, B // 2, 2), :]

    def spread_y(field, into, first=0):
        A, B, _ = field.shape
        into[0:A, pl.ds(first, B, 2), :] = field
        into[0:A, pl.ds(first + 1, B, 2), :] = field

    def twice(field):
        A, B, _ = field.shape
        return jnp.broadcast_to(field[:, None], (A, 2, B, LANES)).reshape(2 * A, B, LANES)

    def own(ref, l, k=None):
        A, B, _ = dims[l]
        return ref[(k,) * (k is not None) + (slice(DEPTH, DEPTH + A), slice(TOP, TOP + B))]

    def beside(ref, a, c, low, rows):
        mid = ref[a:a + c, low:low + rows, :]
        total = ref[a - 1:a - 1 + c, low:low + rows, :] + ref[a + 1:a + 1 + c, low:low + rows, :]
        total = total + ref[a:a + c, low - 1:low - 1 + rows, :] + ref[a:a + c, low + 1:low + 1 + rows, :]
        return mid, total

    def sweep(l, src, rhs, dst, k):
        A, B, _ = dims[l]
        low, rows = TOP - DEPTH, B + 2 * DEPTH
        m = masks[l][...]
        parts = [(k, DEPTH - k, inlow[0])]
        parts += [(a, min(4, DEPTH + A - a), None) for a in range(DEPTH, DEPTH + A, 4)]
        parts += [(DEPTH + A, DEPTH - k, inup[0])]
        for a, c, flag in parts:
            mid, total = beside(src, a, c, low, rows)
            total = total + turn(mid, 1) + turn(mid, -1)
            scale = m if flag is None else m * flag
            dst[a:a + c, low:low + rows, :] = rhs[a:a + c, low:low + rows, :] + (3.0 * mid + total) * scale[None]

    def sweep_slab(src, rhs, dst):
        low, rows = TOP - DEPTH, Y + 2 * DEPTH
        lane = iota((rows, LANES), 1)
        m = ms[...]
        for g in range(groups + 2):
            mid = src[g, low:low + rows, :]
            total = src[g, low - 1:low - 1 + rows, :] + src[g, low + 1:low + 1 + rows, :]
            total = total + turn(mid, 1) + turn(mid, -1)
            before = mid if g == 0 else jnp.where(lane >= LANES - SPAN, src[g - 1, low:low + rows, :], mid)
            after = mid if g == groups + 1 else jnp.where(lane < SPAN, src[g + 1, low:low + rows, :], mid)
            total = total + turn(before, SPAN) + turn(after, -SPAN)
            scale = m * inlow[0] if g == 0 else m * inup[0] if g == groups + 1 else m
            dst[g, low:low + rows, :] = rhs[g, low:low + rows, :] + (3.0 * mid + total) * scale

    def smooth_whole(rhs, width, l):
        A, B, _ = rhs.shape
        lane = iota(rhs.shape, 2)
        e = rhs
        for _ in range(SWEEPS - 1):
            px, py = jnp.zeros((1, B, LANES), jnp.float32), jnp.zeros((A, 1, LANES), jnp.float32)
            total = jnp.concatenate([px, e[:-1]], axis=0) + jnp.concatenate([e[1:], px], axis=0)
            total = total + jnp.concatenate([py, e[:, :-1]], axis=1) + jnp.concatenate([e[:, 1:], py], axis=1)
            total = total + jnp.where(lane == 0, 0.0, turn(e, 1))
            total = total + jnp.where(lane == width - 1, 0.0, turn(e, -1))
            e = rhs + (3.0 * e + total) * (1.0 / 9.0)
        return e * (4.0 ** l / 9.0)

    half, quarter = SPAN // 2, SPAN // 4

    def pack_slab(k):
        lane = iota((Y, LANES), 1)
        line, spot = lane // SPAN, lane % SPAN
        low = high = jnp.zeros((Y, LANES), jnp.float32)
        for g in range(groups):
            both = jnp.zeros((Y, LANES), jnp.float32)
            for i in range(PER):
                field = g0[k, DEPTH + g * PER + i, TOP:TOP + Y, :]
                both = jnp.where((line == i) & (spot < half), turn(field, SPAN * i + quarter), both)
            gs[k, g + 1, TOP:TOP + Y, :] = jnp.where(
                spot < quarter, both, jnp.where(spot >= 3 * quarter, turn(both, half), 0.0))
            here = spot // DEPTH == g
            low = jnp.where(here, turn(both, DEPTH * g - quarter), low)
            high = jnp.where(here, turn(both, DEPTH * g - quarter + DEPTH), high)
        zs[k, 0, 0:Y, :] = low
        zs[k, 1, 0:Y, :] = high

    def pack_level(k, l, first):
        A, B, C = dims[l]
        lane = iota((B, LANES), 1)
        out = jnp.zeros((B, LANES), jnp.float32)
        for i in range(A):
            field = fields[l][k, DEPTH + i, TOP:TOP + B, :]
            out = jnp.where(lane // DEPTH == i, turn(field, DEPTH * i), out)
            out = jnp.where(lane // DEPTH == A + i, turn(field, DEPTH * (A + i) - C + DEPTH), out)
        for side in (0, 1):
            zs[k, side, first:first + B, :] = out

    def unpack_slab(k):
        spot = iota((Y, LANES), 1) % SPAN
        above, below = zr[k, 0, 0:Y, :], zr[k, 1, 0:Y, :]
        for g in range(groups):
            held = gs[k, g + 1, TOP:TOP + Y, :]
            held = jnp.where(spot // DEPTH == 2, turn(above, 2 * DEPTH - DEPTH * g), held)
            gs[k, g + 1, TOP:TOP + Y, :] = jnp.where(spot // DEPTH == 5, turn(below, 5 * DEPTH - DEPTH * g), held)

    def unpack_level(k, l, first):
        A, B, C = dims[l]
        lane = iota((B, LANES), 1)
        above, below = zr[k, 0, first:first + B, :], zr[k, 1, first:first + B, :]
        for i in range(A):
            held = fields[l][k, DEPTH + i, TOP:TOP + B, :]
            held = jnp.where(lane // DEPTH == C // DEPTH, turn(above, C - DEPTH * i), held)
            fields[l][k, DEPTH + i, TOP:TOP + B, :] = jnp.where(
                lane >= LANES - DEPTH, turn(below, -DEPTH - DEPTH * (A + i)), held)

    width = dims[HALOED][2]
    cx, cy, _ = dims[HALOED]
    starts = [0, Y, Y + dims[1][1]]
    packed = cx // plane_groups((cx, cy), width)

    def coarse(k):
        per = plane_groups((cx, cy), width)
        fine = None
        for c in range(nz):
            rows = []
            for i in range(nx):
                columns = []
                for j in range(ny):
                    part = cr[k, (i * ny + j) * nz + c, 0:packed][:, None]
                    part = jnp.broadcast_to(part, (cx // per, per, cy, LANES)).reshape(cx, cy, LANES)
                    columns.append(jnp.where(own_group((cx, cy, LANES), width), part, 0.0))
                rows.append(jnp.concatenate(columns, axis=1))
            spot = lanes_dot(jnp.concatenate(rows, axis=0), gather_matrix(width, c * width))
            fine = spot if fine is None else fine + spot
        chain = [fine]
        widths = [width * nz]
        for l in range(HALOED + 1, LEVELS):
            widths.append(widths[-1] // 2)
            chain.append(lanes_dot(fold_xy(chain[-1]), halve_matrix(widths[-1], 0)))
        whole = smooth_whole(chain[-1], widths[-1], LEVELS - 1)
        for l in range(LEVELS - 2, HALOED - 1, -1):
            i = l - HALOED
            spread_y(whole, spread)
            grown = spread[0:whole.shape[0], 0:2 * whole.shape[1], :]
            grown = twice(lanes_dot(grown, double_matrix(widths[i + 1], 0)))
            whole = grown + smooth_whole(chain[i], widths[i], l)
        wref[DEPTH // 2:DEPTH // 2 + nx * cx, :, :] = whole

    def precondition(k, z, extra):
        start_all(main_copies(k))
        pack_slab(k)
        for l in range(HALOED - 1):
            A, B, C = dims[l + 1]
            fields[l + 1][k, DEPTH:DEPTH + A, TOP:TOP + B, :] = lanes_dot(fold_xy(own(fields[l], l, k)), halve_matrix(C, 0))
            pack_level(k, l + 1, starts[l + 1])
        start_all(z_copies(k))
        mine = lanes_dot(fold_xy(own(fields[HALOED - 1], HALOED - 1, k)), tile_matrix(width))
        mine = jnp.where(own_group(mine.shape, width), mine, 0.0)
        mine = jnp.sum(mine.reshape(-1, plane_groups(mine.shape, width), *mine.shape[1:]), axis=1)
        mine = jnp.sum(mine, axis=1, keepdims=True)
        mine = jnp.concatenate([mine, extra], axis=0)
        cs[k] = mine
        cr[k, me] = mine
        to_all(cs.at[k], cr.at[k], csend.at[k], crecv.at[k])
        wait_all(z_copies(k))
        unpack_slab(k)
        for l in range(1, HALOED):
            unpack_level(k, l, starts[l])
        start_more(k)
        wait_all(main_copies(k))
        for s in range(1, SWEEPS):
            src = g0.at[k] if s == 1 else ping[0][s % 2]
            sweep(0, src, g0.at[k], ping[0][(s + 1) % 2], s)
        wait_more(k)
        for s in range(1, SWEEPS):
            src = gs.at[k] if s == 1 else (fsa, fsb)[s % 2]
            sweep_slab(src, gs.at[k], (fsa, fsb)[(s + 1) % 2])
            for l in range(1, HALOED):
                src = fields[l].at[k] if s == 1 else ping[l][s % 2]
                sweep(l, src, fields[l].at[k], ping[l][(s + 1) % 2], s)
        all_done(cr.at[k], crecv.at[k])
        coarse(k)
        last = SWEEPS % 2
        spread_y(wref[pl.ds(at[0] * cx, cx + DEPTH)], wide, DEPTH)
        part = wide[:, pl.ds(pl.multiple_of(at[1] * 2 * cy, 8), 2 * cy + 2 * DEPTH), :]
        part = lanes_dot(part, double_around(at[2] * width, width * nz, dims[HALOED - 1][2]))
        part = twice(part)[DEPTH - 1:DEPTH + dims[HALOED - 1][0] + 1]
        for l in range(HALOED - 1, 0, -1):
            A, B, C = dims[l]
            end = ping[l][last][DEPTH - 1:DEPTH + A + 1, TOP - DEPTH:TOP + B + DEPTH, :]
            full = end * (4.0 ** l / 9.0) + part
            if l > 1:
                spread_y(lanes_dot(full, double_around(0, None, dims[l - 1][2])), spread)
                part = twice(spread[0:A + 2, DEPTH:DEPTH + 2 * B + 2 * DEPTH, :])[1:2 * A + 3]
            else:
                spread_y(lanes_dot(full, double_matrix(C, 0)), pd)
                spread_y(lanes_dot(full, ends_matrix(C)), pe)
        low, rows = TOP - DEPTH, Y + 2 * DEPTH
        slab = (fsa, fsb)[last]
        spot = iota((rows, LANES), 1) % SPAN
        for g in range(groups + 2):
            s = slab[g, low:low + rows, :]
            sc[g] = jnp.where(spot < quarter, s, turn(s, -half))
            sd[g] = jnp.where(spot <= quarter, s, turn(s, quarter + 1 - (3 * quarter - 1)))
        lane = iota((rows, LANES), 1)
        near = (lane < DEPTH - 1) | (lane > LANES - DEPTH)
        end = ping[0][last]
        for p in range(DEPTH - 1, DEPTH + X + 1):
            g, i = p // PER, p % PER
            f = jnp.where(near, turn(sc[g], -quarter - SPAN * i), end[p, low:low + rows, :])
            z[p, low:low + rows, :] = f * (1.0 / 9.0) + pd[(p - DEPTH + 2) // 2, low:low + rows, :]

    def operator(z, p):
        lane = iota((Y, LANES), 1)
        mid, total = beside(z, p, 1, TOP, Y)
        mid, total = mid[0], total[0]
        g, i = p // PER, p % PER
        ghost = turn(sd[g, DEPTH:DEPTH + Y, :], LANES - 1 - quarter - SPAN * i) * (1.0 / 9.0)
        ghost = ghost + pe[(p - DEPTH + 2) // 2, TOP:TOP + Y, :]
        total = total + jnp.where(lane == 0, ghost, turn(mid, 1))
        total = total + jnp.where(lane == LANES - 1, ghost, turn(mid, -1))
        return mid, 6.0 * mid - total

    load_x.wait()
    lane = iota((Y, LANES), 1)
    out = jnp.zeros((Y, LANES), jnp.float32)
    for i in range(X):
        out = jnp.where(lane // 2 == i, turn(ux[1 + i, TOP:TOP + Y, :], 2 * i + 1), out)
    ze[...] = out
    pl.semaphore_wait(barrier, n - 1)
    start_all(face_copies())
    load_b.wait()
    wait_all(face_copies())
    ghosts = jnp.where(lane % 2 == 0, turn(zi[1], -1), turn(zi[0], 1))
    for i in range(X):
        mid, total = beside(ux, 1 + i, 1, TOP, Y)
        mid, total = mid[0], total[0]
        ghost = turn(ghosts, -2 * i - 1)
        total = total + jnp.where(lane == 0, ghost, turn(mid, 1))
        total = total + jnp.where(lane == LANES - 1, ghost, turn(mid, -1))
        g0[0, DEPTH + i, TOP:TOP + Y, :] = bb[i] - (6.0 * mid - total)

    def sums_of(a, b):
        return jnp.concatenate([jnp.sum(a, axis=0, keepdims=True), jnp.sum(b, axis=0, keepdims=True)], axis=0)

    def ratio(parts):
        both = jnp.sum(parts, axis=0)
        both = jnp.sum(both, axis=1, keepdims=True)
        return both[0:1] / both[1:2]

    nothing = jnp.zeros((Y, LANES), jnp.float32)
    precondition(0, z0, jnp.zeros((2, 1, LANES), jnp.float32))
    rz, zw = nothing, nothing
    for i in range(X):
        mid, image = operator(z0, DEPTH + i)
        g0[1, DEPTH + i, TOP:TOP + Y, :] = image
        rz = rz + g0[0, DEPTH + i, TOP:TOP + Y, :] * mid
        zw = zw + mid * image
    precondition(1, z1, sums_of(rz, zw)[:, None, :])
    alpha = ratio(cr[1, :, packed:packed + 2, 0, :])
    rz, zw = nothing, nothing
    for i in range(X):
        mid, image = operator(z1, DEPTH + i)
        here = (DEPTH + i, slice(TOP, TOP + Y))
        zi0, w0 = z0[here], g0[(1,) + here]
        r = g0[(0,) + here] - alpha * w0
        zi1 = zi0 - alpha * mid
        w1 = w0 - alpha * image
        rz = rz + r * zi1
        zw = zw + zi1 * w1
        sol_ref[i] = ux[1 + i, TOP:TOP + Y, :] + alpha * zi0
        res_ref[i] = r
        bb[i] = zi1
        wv[i] = w1
    sums = sums_of(rz, zw)
    ds[...] = sums
    dr[me] = sums
    to_all(ds, dr, dsend.at[0], drecv.at[0])
    sent_all(face_copies())
    for k in range(STEPS):
        sent_all(z_copies(k))
        sent_all(main_copies(k))
        sent_more(k)
        all_done(cr.at[k], csend.at[k])
    all_done(dr, drecv.at[0])
    alpha = ratio(dr[...])
    for i in range(X):
        sol_ref[i] = sol_ref[i] + alpha * bb[i]
        res_ref[i] = res_ref[i] - alpha * wv[i]
    all_done(dr, dsend.at[0])


def solution(mesh):
    sizes = tuple(mesh.shape[a] for a in AXES)
    n = sizes[0] * sizes[1] * sizes[2]

    def run(right_side, guess):
        X, Y, Z = block = guess.shape
        assert Z == LANES and PER == DEPTH and X % PER == 0 and X * DEPTH <= LANES
        dims = [tuple(d >> l for d in block) for l in range(LEVELS)]
        f32 = jnp.float32
        vm = lambda *s: pltpu.VMEM(s, f32)
        ext = [(dims[l][0] + 2 * DEPTH, dims[l][1] + 2 * TOP, LANES) for l in range(HALOED)]
        slab = (X // PER + 2, Y + 2 * TOP, LANES)
        tall = [(dims[l][1] + 2 * DEPTH, LANES) for l in range(HALOED)]
        cx, cy, width = dims[HALOED]
        packed = cx // plane_groups((cx, cy), width) + 2
        zrows = sum(dims[l][1] for l in range(HALOED))
        dma = lambda *s: pltpu.SemaphoreType.DMA(s)
        scratch = [
            vm(X + 2, Y + 2 * TOP, LANES), vm(*block),
            *(vm(STEPS, *e) for e in ext), vm(STEPS, *slab),
            *(vm(*e) for e in ext for _ in range(2)), vm(*slab), vm(*slab),
            vm(*ext[0]), vm(*ext[0]), vm(*block),
            vm(slab[0], *tall[0]), vm(slab[0], *tall[0]),
            vm(dims[1][0] + 2, 2 * tall[1][0], LANES), vm(dims[1][0] + 2, 2 * tall[1][0], LANES),
            *(vm(*t) for t in tall), vm(*tall[0]),
            vm(cx * sizes[0] + DEPTH, cy * sizes[1], LANES),
            vm(cx + DEPTH, 2 * cy * sizes[1] + 2 * DEPTH, LANES),
            vm(X // 2, Y, LANES), vm(X // 2, 2 * Y, LANES),
            vm(Y, LANES), vm(2, Y, LANES),
            vm(STEPS, 2, zrows, LANES), vm(STEPS, 2, zrows, LANES),
            vm(STEPS, packed, 1, LANES), vm(STEPS, n, packed, 1, LANES),
            vm(2, LANES), vm(n, 2, LANES),
            dma(2), dma(6), dma(6), dma(STEPS, 2), dma(STEPS, 2),
            dma(STEPS, 8), dma(STEPS, 8), dma(STEPS, HALOED, 8), dma(STEPS, HALOED, 8),
            dma(STEPS), dma(STEPS), dma(1), dma(1),
        ]
        return tuple(pl.pallas_call(
            functools.partial(kernel, sizes, block),
            out_shape=(pltpu.VMEM(block, f32), pltpu.VMEM(block, f32)),
            in_specs=[pl.BlockSpec(memory_space=pl.ANY)] * 2,
            out_specs=[pl.BlockSpec(memory_space=pltpu.VMEM)] * 2,
            scratch_shapes=scratch,
            compiler_params=pltpu.CompilerParams(collective_id=0, has_side_effects=True),
        )(right_side, guess))

    spec = P(*AXES)
    return jax.shard_map(run, mesh=mesh, in_specs=(spec, spec), out_specs=(spec, spec), check_vma=False)
```

time: 65.8 us -> 42 us (0.64)
  Pallas kernels: 62.2 us -> 39.6 us
  local copies, waits for them, and re-layouts: 2.72 us -> 1.59 us
    pallas_call x1, Pallas kernels: 62.2 us -> 39.6 us  [run(): pl.pallas_call(functools.partial(kernel, sizes, block), out_shape=(pltpu....]
    unnamed x4 -> x2, local copies, waits for them, and re-layouts: 2.72 us -> 1.59 us
where the time goes in v1:
time: 42 us; the launch traced here: 41.8 us
  Pallas kernels  39.6 us (94%)
  local copies, waits for them, and re-layouts  1.59 us (4%)
  between operations  0.64 us (2%)
    pallas_call x1, Pallas kernels, run(): pl.pallas_call(functools.partial(kernel, sizes, block), out_shape=(pltpu....  39.6 us
    unnamed x2, local copies, waits for them, and re-layouts  1.59 us

profile of v1, /device:TPU:0, one launch (start us, length us, event | category | flops | bytes accessed | tf_op | source)
XLA Modules:
  0.0 41.8 jit_solution(17024096396371488908)
XLA Ops:
  0.6 39.6 %shard_map.41 = (f32[32,32,128]{2,1,0:T(8,128)S(1)}, f32[32,32,128]{2,1,0:T(8,128)S(1)}) custom-call(f32[32,32,128]{2,1,0:T(8,128)} %b_hbm.1, f32[32,32,128]{2,1,0:T(8,128)} %x_hbm.1), custom_call_target="tpu_custom_call" | custom-call | tf_op jit(solution)/shard_map/pallas_call | solution.py:597
  40.2 0.8 %copy.6 = f32[32,32,128]{2,1,0:T(8,128)} copy(f32[32,32,128]{2,1,0:T(8,128)S(1)} %get-tuple-element.2) | data formatting | bytes 1048576
  41.0 0.8 %copy.7 = f32[32,32,128]{2,1,0:T(8,128)} copy(f32[32,32,128]{2,1,0:T(8,128)S(1)} %get-tuple-element.3) | data formatting | bytes 1048576

commit v2 on v1

--- a/solution.py
+++ b/solution.py
@@ -36,6 +36,13 @@
     return jnp.concatenate(planes, axis=0)
 
 
+def take(x, index):
+    index = jnp.broadcast_to(index[:1], x.shape[-2:])
+    if x.ndim == 2:
+        return jnp.take_along_axis(x, index, axis=1, mode="promise_in_bounds")
+    return jnp.stack([jnp.take_along_axis(x[i], index, axis=1, mode="promise_in_bounds") for i in range(x.shape[0])])
+
+
 def halve_matrix(width, start):
     source, target = iota((LANES, LANES), 0), iota((LANES, LANES), 1) - start
     keep = (target >= 0) & (target < width) & ((source == 2 * target) | (source == 2 * target + 1))
@@ -52,21 +59,9 @@
     return jnp.where(lane >= LANES - DEPTH, lane - LANES, lane)
 
 
-def double_around(coarse_start, coarse_total, fine_width):
-    source, target = iota((LANES, LANES), 0), wrapped(iota((LANES, LANES), 1))
-    at = (target >> 1) + coarse_start
-    if coarse_total is None:
-        at = at & (LANES - 1)
-        keep = (source == at) & (target < fine_width + DEPTH)
-    else:
-        keep = (source == at) & (target < fine_width + DEPTH) & (source < coarse_total)
-    return jnp.where(keep, 1.0, 0.0)
-
-
-def ends_matrix(width):
-    source, target = iota((LANES, LANES), 0), iota((LANES, LANES), 1)
-    keep = ((target == 0) & (source == LANES - 1)) | ((target == LANES - 1) & (source == width))
-    return jnp.where(keep, 1.0, 0.0)
+def halve(x, width):
+    lane = iota((8, LANES), 1)
+    return take(x + turn(x, -1), 2 * (lane % width)) * 0.125
 
 
 def plane_groups(shape, width):
@@ -78,11 +73,6 @@
     return iota(shape, 2) // width == group
 
 
-def tile_matrix(width):
-    source, target = iota((LANES, LANES), 0), iota((LANES, LANES), 1) % width
-    return jnp.where((source == 2 * target) | (source == 2 * target + 1), 0.125, 0.0)
-
-
 def gather_matrix(width, start):
     source, target = iota((LANES, LANES), 0) % width, iota((LANES, LANES), 1) - start
     return jnp.where(source == target, 1.0, 0.0)
@@ -93,10 +83,10 @@
     return pltpu.roll(x, shift, x.ndim - 1) if shift else x
 
 
-def kernel(sizes, block, b_hbm, x_hbm, sol_ref, res_ref, *rest):
-    (ux, bb, g0, g1, g2, gs, f0a, f0b, f1a, f1b, f2a, f2b, fsa, fsb, z0, z1, wv, sc, sd, pd, pe,
-     m0, m1, m2, ms, wref, wide, fold, spread, ze, zi, zs, zr, cs, cr, ds, dr,
-     isem, xsend, xrecv, zsend, zrecv, msend, mrecv, fsend, frecv, csend, crecv, dsend, drecv) = rest
+def kernel(sizes, block, b_hbm, x_hbm, sol_ref, z_ref, res_ref, w_ref, alpha_ref, *rest):
+    (ux, bb, g0, g1, g2, gs, f0a, f0b, f0c, f1a, f1b, f1c, f2a, f2b, f2c, fsa, fsb, fsc, z0, z1, sc, sd, pd, pe,
+     m0, m1, m2, ms, wref, wide, fold, spread, xg, yg, ze, zi, zs, zr, cs, cr, ds, dr, blank,
+     isem, xsend, xrecv, zsend, zrecv, send, mrecv, frecv, csend, crecv, dsend, drecv) = rest
     nx, ny, nz = sizes
     n = nx * ny * nz
     at = tuple(lax.axis_index(a) for a in AXES)
@@ -104,7 +94,7 @@
     dims = [tuple(d >> l for d in block) for l in range(LEVELS)]
     X, Y, Z = block
     fields = (g0, g1, g2)
-    ping = ((f0a, f0b), (f1a, f1b), (f2a, f2b))
+    after = ((f0a, f0b, f0c), (f1a, f1b, f1c), (f2a, f2b, f2c), (fsa, fsb, fsc))
     masks = (m0, m1, m2)
     groups = X // PER
     lower = [at[d] > 0 for d in range(3)]
@@ -121,28 +111,39 @@
         moved = [[lax.rem(at[d] + k, sizes[d]) if k else at[d] for k in range(sizes[d])] for d in range(3)]
         return [(a, b, c) for a in moved[0] for b in moved[1] for c in moved[2]][1:]
 
-    def clear(ref, lead, planes, depth, rows, own):
-        zero = jnp.float32(0)
-        for i in lead:
-            head = (i,) if i is not None else ()
-            for a, b in ((0, depth), (planes - depth, planes)):
-                ref[head + (slice(a, b),)] = jnp.full((b - a,) + ref.shape[-2:], zero)
-            for a, b in ((0, TOP), (TOP + own, rows)):
-                ref[head + (slice(depth, planes - depth), slice(a, b))] = jnp.full((planes - 2 * depth, b - a, LANES), zero)
-
-    clear(ux, (None,), X + 2, 1, Y + 2 * TOP, Y)
-    for l in range(HALOED):
-        clear(fields[l], range(STEPS), dims[l][0] + 2 * DEPTH, DEPTH, dims[l][1] + 2 * TOP, dims[l][1])
-    clear(gs, range(STEPS), groups + 2, 1, Y + 2 * TOP, Y)
-    zi[...] = jnp.zeros_like(zi)
-    zr[...] = jnp.zeros_like(zr)
-
     barrier = pltpu.get_barrier_semaphore()
     for target in others():
         pl.semaphore_signal(barrier, inc=1, device_id=target, device_id_type=MESH)
 
-    for ref in (f0a, f0b, f1a, f1b, f2a, f2b, fsa, fsb):
-        ref[...] = jnp.zeros_like(ref)
+    def outside(dim, side):
+        for l in range(HALOED + 1):
+            A, B = (groups if l == HALOED else dims[l][0]), (Y if l == HALOED else dims[l][1])
+            d, ref = (1, gs) if l == HALOED else (DEPTH, fields[l])
+            for k in range(STEPS):
+                if dim == 0:
+                    a = A + d if side else 0
+                    ref[k, a:a + d, TOP - DEPTH:TOP + B + DEPTH, :] = jnp.zeros((d, B + 2 * DEPTH, LANES), jnp.float32)
+                else:
+                    a = TOP + B if side else TOP - DEPTH
+                    ref[k, :, a:a + DEPTH, :] = jnp.zeros((A + 2 * d, DEPTH, LANES), jnp.float32)
+
+    for side in (0, 1):
+        for dim in range(2):
+            @pl.when(jnp.logical_not((upper if side else lower)[dim]))
+            def _(dim=dim, side=side):
+                outside(dim, side)
+                ref = (xg, yg)[dim]
+                ref[1 - side] = jnp.zeros(ref.shape[1:], jnp.float32)
+        @pl.when(jnp.logical_not((upper if side else lower)[2]))
+        def _(side=side):
+            zi[1 if side else 0] = jnp.zeros(zi.shape[1:], jnp.float32)
+            for k in range(STEPS):
+                zr[k, 0 if side else 1] = jnp.zeros(zr.shape[2:], jnp.float32)
+
+    ux[:, TOP - 1:TOP, :] = jnp.zeros((X + 2, 1, LANES), jnp.float32)
+    ux[:, TOP + Y:TOP + Y + 1, :] = jnp.zeros((X + 2, 1, LANES), jnp.float32)
+    ux[0, TOP:TOP + Y, :] = jnp.zeros((Y, LANES), jnp.float32)
+    ux[X + 1, TOP:TOP + Y, :] = jnp.zeros((Y, LANES), jnp.float32)
     wref[...] = jnp.zeros_like(wref)
     wide[...] = jnp.zeros_like(wide)
 
@@ -162,12 +163,12 @@
         for i, (d, s) in enumerate(FACES):
             target = list(at)
             target[d] = at[d] + s
+            into = 1 if s > 0 else 0
             if d == 0:
-                src, dst = (X, 0) if s > 0 else (1, X + 1)
-                src, dst = ux.at[src:src + 1, TOP:TOP + Y], ux.at[dst:dst + 1, TOP:TOP + Y]
+                src, dst = ux.at[X if s > 0 else 1, TOP:TOP + Y], xg.at[into]
             elif d == 1:
-                src, dst = (TOP + Y - 1, TOP - 1) if s > 0 else (TOP, TOP + Y)
-                src, dst = ux.at[1:X + 1, src:src + 1], ux.at[1:X + 1, dst:dst + 1]
+                a = TOP + Y - 1 if s > 0 else TOP
+                src, dst = ux.at[1:X + 1, a:a + 1], yg.at[into]
             else:
                 src, dst = ze, zi.at[0 if s > 0 else 1]
             copy = pltpu.make_async_remote_copy(
@@ -181,7 +182,7 @@
         out = []
         for side in (0, 1):
             copy = pltpu.make_async_remote_copy(
-                src_ref=zs.at[k, side], dst_ref=zr.at[k, side], send_sem=zsend.at[k, side], recv_sem=zrecv.at[k, side],
+                src_ref=zs.at[k, side], dst_ref=zr.at[k, side], send_sem=zsend.at[side], recv_sem=zrecv.at[k, side],
                 device_id=(at[0], at[1], at[2] + (1 if side else -1)), device_id_type=MESH,
             )
             out.append((copy, upper[2] if side else lower[2], lower[2] if side else upper[2]))
@@ -194,14 +195,14 @@
             return (start, depth), (start + own, depth)
         return (start, own), (start, own)
 
-    def around_copies(ref, k, depth, planes, rows, ssem, rsem):
+    def around_copies(ref, k, depth, planes, rows, rsem):
         out = []
         for i, (dx, dy) in enumerate(AROUND):
             (sx, lx), (tx, _) = span(dx, depth, depth, planes, None)
             (sy, ly), (ty, _) = span(dy, DEPTH, TOP, rows, None)
             copy = pltpu.make_async_remote_copy(
                 src_ref=ref.at[k, sx:sx + lx, sy:sy + ly], dst_ref=ref.at[k, tx:tx + lx, ty:ty + ly],
-                send_sem=ssem(i), recv_sem=rsem(i),
+                send_sem=send.at[i], recv_sem=rsem.at[k, i],
                 device_id=(at[0] + dx, at[1] + dy, at[2]), device_id_type=MESH,
             )
             to, fro = None, None
@@ -210,52 +211,56 @@
                     a, b = (upper[d], lower[d]) if s > 0 else (lower[d], upper[d])
                     to = a if to is None else jnp.logical_and(to, a)
                     fro = b if fro is None else jnp.logical_and(fro, b)
-            out.append((copy, to, fro))
+            out.append((copy, to, fro, lx * ly))
         return out
 
     def main_copies(k):
-        return around_copies(g0, k, DEPTH, X, Y, lambda i: msend.at[k, i], lambda i: mrecv.at[k, i])
+        return around_copies(g0, k, DEPTH, X, Y, mrecv)
 
     def more_copies(k):
-        out = [around_copies(gs, k, 1, groups, Y, lambda i: fsend.at[k, 0, i], lambda i: frecv.at[k, 0, i])]
+        out = [around_copies(gs, k, 1, groups, Y, frecv)]
         for l in range(1, HALOED):
-            out.append(around_copies(
-                fields[l], k, DEPTH, dims[l][0], dims[l][1],
-                lambda i, l=l: fsend.at[k, l, i], lambda i, l=l: frecv.at[k, l, i]))
+            out.append(around_copies(fields[l], k, DEPTH, dims[l][0], dims[l][1], frecv))
         return [[kind[i] for kind in out] for i in range(len(AROUND))]
 
+    def lines(copies):
+        return sum(entry[3] for entry in copies)
+
+    def bytes_done(count, sem):
+        part = blank.at[pl.ds(0, count)]
+        pltpu.make_async_copy(part, part, sem).wait()
+
     def start_all(copies):
-        for copy, cond, _ in copies:
+        for copy, cond, *_ in copies:
             pl.when(cond)(copy.start)
 
     def wait_all(copies):
-        for copy, _, cond in copies:
+        for copy, _, cond, *_ in copies:
             pl.when(cond)(copy.wait_recv)
 
     def sent_all(copies):
-        for copy, cond, _ in copies:
+        for copy, cond, *_ in copies:
             pl.when(cond)(copy.wait_send)
 
     def start_more(k):
         for same in more_copies(k):
             @pl.when(same[0][1])
             def _(same=same):
-                for copy, _, _ in same:
+                for copy, *_ in same:
                     copy.start()
 
     def wait_more(k):
-        for same in more_copies(k):
-            @pl.when(same[0][2])
-            def _(same=same):
-                for copy, _, _ in same:
-                    copy.wait_recv()
-
-    def sent_more(k):
-        for same in more_copies(k):
-            @pl.when(same[0][1])
-            def _(same=same):
-                for copy, _, _ in same:
-                    copy.wait_send()
+        for i, same in enumerate(more_copies(k)):
+            pl.when(same[0][2])(lambda i=i, same=same: bytes_done(lines(same), frecv.at[k, i]))
+
+    def sent_around():
+        for i, same in enumerate(more_copies(0)):
+            count = STEPS * (lines(same) + lines([main_copies(0)[i]]))
+            pl.when(same[0][1])(lambda i=i, count=count: bytes_done(count, send.at[i]))
+        for side in (0, 1):
+            part = zs.at[:, side]
+            cond = upper[2] if side else lower[2]
+            pl.when(cond)(pltpu.make_async_copy(part, part, zsend.at[side]).wait)
 
     def to_all(src, dst, s_sem, r_sem):
         for target in others():
@@ -287,24 +292,41 @@
         A, B, _ = dims[l]
         return ref[(k,) * (k is not None) + (slice(DEPTH, DEPTH + A), slice(TOP, TOP + B))]
 
-    def beside(ref, a, c, low, rows):
-        mid = ref[a:a + c, low:low + rows, :]
-        total = ref[a - 1:a - 1 + c, low:low + rows, :] + ref[a + 1:a + 1 + c, low:low + rows, :]
-        total = total + ref[a:a + c, low - 1:low - 1 + rows, :] + ref[a:a + c, low + 1:low + 1 + rows, :]
-        return mid, total
+    def update(src, rhs, dst, a, c, low, rows, scale):
+        at_rows = slice(low, low + rows)
+        mid = src[a:a + c, at_rows, :]
+        total = src[a - 1:a - 1 + c, at_rows, :] + src[a + 1:a + 1 + c, at_rows, :]
+        total = total + src[a:a + c, low - 1:low - 1 + rows, :] + src[a:a + c, low + 1:low + 1 + rows, :]
+        total = total + turn(mid, 1) + turn(mid, -1)
+        dst[a:a + c, at_rows, :] = rhs[a:a + c, at_rows, :] + (3.0 * mid + total) * scale
+
+    def pieces(a, b):
+        return [(p, min(4, b - p)) for p in range(a, b, 4)]
 
     def sweep(l, src, rhs, dst, k):
         A, B, _ = dims[l]
         low, rows = TOP - DEPTH, B + 2 * DEPTH
         m = masks[l][...]
-        parts = [(k, DEPTH - k, inlow[0])]
-        parts += [(a, min(4, DEPTH + A - a), None) for a in range(DEPTH, DEPTH + A, 4)]
-        parts += [(DEPTH + A, DEPTH - k, inup[0])]
-        for a, c, flag in parts:
-            mid, total = beside(src, a, c, low, rows)
-            total = total + turn(mid, 1) + turn(mid, -1)
-            scale = m if flag is None else m * flag
-            dst[a:a + c, low:low + rows, :] = rhs[a:a + c, low:low + rows, :] + (3.0 * mid + total) * scale[None]
+        update(src, rhs, dst, k, DEPTH - k, low, rows, m * inlow[0])
+        for a, c in pieces(DEPTH, DEPTH + A):
+            update(src, rhs, dst, a, c, low, rows, m)
+        update(src, rhs, dst, DEPTH + A, DEPTH - k, low, rows, m * inup[0])
+
+    def sweep_inside(src, rhs, dst, k):
+        for a, c in pieces(DEPTH + k, DEPTH + X - k):
+            update(src, rhs, dst, a, c, TOP + k, Y - 2 * k, 1.0 / 9.0)
+
+    def sweep_rim(src, rhs, dst, k):
+        low, rows = TOP - DEPTH, Y + 2 * DEPTH
+        m = m0[...]
+        update(src, rhs, dst, k, DEPTH - k, low, rows, m * inlow[0])
+        update(src, rhs, dst, DEPTH, k, low, rows, m)
+        update(src, rhs, dst, DEPTH + X - k, k, low, rows, m)
+        update(src, rhs, dst, DEPTH + X, DEPTH - k, low, rows, m * inup[0])
+        for start in (0, Y):
+            edge = m0[start:start + 2 * DEPTH, :]
+            for a, c in pieces(DEPTH + k, DEPTH + X - k):
+                update(src, rhs, dst, a, c, low + start, 2 * DEPTH, edge)
 
     def sweep_slab(src, rhs, dst):
         low, rows = TOP - DEPTH, Y + 2 * DEPTH
@@ -315,8 +337,8 @@
             total = src[g, low - 1:low - 1 + rows, :] + src[g, low + 1:low + 1 + rows, :]
             total = total + turn(mid, 1) + turn(mid, -1)
             before = mid if g == 0 else jnp.where(lane >= LANES - SPAN, src[g - 1, low:low + rows, :], mid)
-            after = mid if g == groups + 1 else jnp.where(lane < SPAN, src[g + 1, low:low + rows, :], mid)
-            total = total + turn(before, SPAN) + turn(after, -SPAN)
+            behind = mid if g == groups + 1 else jnp.where(lane < SPAN, src[g + 1, low:low + rows, :], mid)
+            total = total + turn(before, SPAN) + turn(behind, -SPAN)
             scale = m * inlow[0] if g == 0 else m * inup[0] if g == groups + 1 else m
             dst[g, low:low + rows, :] = rhs[g, low:low + rows, :] + (3.0 * mid + total) * scale
 
@@ -404,25 +426,27 @@
         widths = [width * nz]
         for l in range(HALOED + 1, LEVELS):
             widths.append(widths[-1] // 2)
-            chain.append(lanes_dot(fold_xy(chain[-1]), halve_matrix(widths[-1], 0)))
+            chain.append(jnp.where(iota((1, 1, LANES), 2) < widths[-1], halve(fold_xy(chain[-1]), LANES // 2), 0.0))
         whole = smooth_whole(chain[-1], widths[-1], LEVELS - 1)
         for l in range(LEVELS - 2, HALOED - 1, -1):
             i = l - HALOED
             spread_y(whole, spread)
             grown = spread[0:whole.shape[0], 0:2 * whole.shape[1], :]
-            grown = twice(lanes_dot(grown, double_matrix(widths[i + 1], 0)))
+            grown = twice(take(grown, iota((8, LANES), 1) // 2))
             whole = grown + smooth_whole(chain[i], widths[i], l)
         wref[DEPTH // 2:DEPTH // 2 + nx * cx, :, :] = whole
 
     def precondition(k, z, extra):
         start_all(main_copies(k))
-        pack_slab(k)
+        lane = iota((8, LANES), 1)
         for l in range(HALOED - 1):
             A, B, C = dims[l + 1]
-            fields[l + 1][k, DEPTH:DEPTH + A, TOP:TOP + B, :] = lanes_dot(fold_xy(own(fields[l], l, k)), halve_matrix(C, 0))
+            coarser = jnp.where(iota((1, 1, LANES), 2) < C, halve(fold_xy(own(fields[l], l, k)), LANES // 2), 0.0)
+            fields[l + 1][k, DEPTH:DEPTH + A, TOP:TOP + B, :] = coarser
             pack_level(k, l + 1, starts[l + 1])
+        pack_slab(k)
         start_all(z_copies(k))
-        mine = lanes_dot(fold_xy(own(fields[HALOED - 1], HALOED - 1, k)), tile_matrix(width))
+        mine = halve(fold_xy(own(fields[HALOED - 1], HALOED - 1, k)), width)
         mine = jnp.where(own_group(mine.shape, width), mine, 0.0)
         mine = jnp.sum(mine.reshape(-1, plane_groups(mine.shape, width), *mine.shape[1:]), axis=1)
         mine = jnp.sum(mine, axis=1, keepdims=True)
@@ -430,6 +454,8 @@
         cs[k] = mine
         cr[k, me] = mine
         to_all(cs.at[k], cr.at[k], csend.at[k], crecv.at[k])
+        for s in range(1, SWEEPS):
+            sweep_inside(after[0][s - 2] if s > 1 else g0.at[k], g0.at[k], after[0][s - 1], s)
         wait_all(z_copies(k))
         unpack_slab(k)
         for l in range(1, HALOED):
@@ -437,34 +463,33 @@
         start_more(k)
         wait_all(main_copies(k))
         for s in range(1, SWEEPS):
-            src = g0.at[k] if s == 1 else ping[0][s % 2]
-            sweep(0, src, g0.at[k], ping[0][(s + 1) % 2], s)
+            sweep_rim(after[0][s - 2] if s > 1 else g0.at[k], g0.at[k], after[0][s - 1], s)
+        all_done(cr.at[k], crecv.at[k])
+        coarse(k)
+        spread_y(wref[pl.ds(at[0] * cx, cx + DEPTH)], wide, DEPTH)
+        part = wide[:, pl.ds(pl.multiple_of(at[1] * 2 * cy, 8), 2 * cy + 2 * DEPTH), :]
+        source = (wrapped(lane) >> 1) + at[2] * width
+        inside = (source >= 0) & (source < width * nz)
+        part = take(part, jnp.where(inside, source, 0))
+        part = jnp.where(inside[0:1][None], part, 0.0)
+        part = twice(part)[DEPTH - 1:DEPTH + dims[HALOED - 1][0] + 1]
         wait_more(k)
         for s in range(1, SWEEPS):
-            src = gs.at[k] if s == 1 else (fsa, fsb)[s % 2]
-            sweep_slab(src, gs.at[k], (fsa, fsb)[(s + 1) % 2])
+            sweep_slab(after[3][s - 2] if s > 1 else gs.at[k], gs.at[k], after[3][s - 1])
             for l in range(1, HALOED):
-                src = fields[l].at[k] if s == 1 else ping[l][s % 2]
-                sweep(l, src, fields[l].at[k], ping[l][(s + 1) % 2], s)
-        all_done(cr.at[k], crecv.at[k])
-        coarse(k)
-        last = SWEEPS % 2
-        spread_y(wref[pl.ds(at[0] * cx, cx + DEPTH)], wide, DEPTH)
-        part = wide[:, pl.ds(pl.multiple_of(at[1] * 2 * cy, 8), 2 * cy + 2 * DEPTH), :]
-        part = lanes_dot(part, double_around(at[2] * width, width * nz, dims[HALOED - 1][2]))
-        part = twice(part)[DEPTH - 1:DEPTH + dims[HALOED - 1][0] + 1]
+                sweep(l, after[l][s - 2] if s > 1 else fields[l].at[k], fields[l].at[k], after[l][s - 1], s)
         for l in range(HALOED - 1, 0, -1):
             A, B, C = dims[l]
-            end = ping[l][last][DEPTH - 1:DEPTH + A + 1, TOP - DEPTH:TOP + B + DEPTH, :]
+            end = after[l][SWEEPS - 2][DEPTH - 1:DEPTH + A + 1, TOP - DEPTH:TOP + B + DEPTH, :]
             full = end * (4.0 ** l / 9.0) + part
             if l > 1:
-                spread_y(lanes_dot(full, double_around(0, None, dims[l - 1][2])), spread)
+                spread_y(take(full, (wrapped(lane) >> 1) & (LANES - 1)), spread)
                 part = twice(spread[0:A + 2, DEPTH:DEPTH + 2 * B + 2 * DEPTH, :])[1:2 * A + 3]
             else:
-                spread_y(lanes_dot(full, double_matrix(C, 0)), pd)
-                spread_y(lanes_dot(full, ends_matrix(C)), pe)
+                spread_y(take(full, lane // 2), pd)
+                spread_y(take(full, jnp.where(lane == 0, LANES - 1, C)), pe)
         low, rows = TOP - DEPTH, Y + 2 * DEPTH
-        slab = (fsa, fsb)[last]
+        slab = after[3][SWEEPS - 2]
         spot = iota((rows, LANES), 1) % SPAN
         for g in range(groups + 2):
             s = slab[g, low:low + rows, :]
@@ -472,25 +497,30 @@
             sd[g] = jnp.where(spot <= quarter, s, turn(s, quarter + 1 - (3 * quarter - 1)))
         lane = iota((rows, LANES), 1)
         near = (lane < DEPTH - 1) | (lane > LANES - DEPTH)
-        end = ping[0][last]
+        end = after[0][SWEEPS - 2]
         for p in range(DEPTH - 1, DEPTH + X + 1):
             g, i = p // PER, p % PER
             f = jnp.where(near, turn(sc[g], -quarter - SPAN * i), end[p, low:low + rows, :])
             z[p, low:low + rows, :] = f * (1.0 / 9.0) + pd[(p - DEPTH + 2) // 2, low:low + rows, :]
 
+    def around(ref, p):
+        mid = ref[p, TOP:TOP + Y, :]
+        total = ref[p - 1, TOP:TOP + Y, :] + ref[p + 1, TOP:TOP + Y, :]
+        return mid, total + ref[p, TOP - 1:TOP - 1 + Y, :] + ref[p, TOP + 1:TOP + 1 + Y, :]
+
+    lane = iota((Y, LANES), 1)
+    first, last = lane == 0, lane == LANES - 1
+
     def operator(z, p):
-        lane = iota((Y, LANES), 1)
-        mid, total = beside(z, p, 1, TOP, Y)
-        mid, total = mid[0], total[0]
+        mid, total = around(z, p)
         g, i = p // PER, p % PER
         ghost = turn(sd[g, DEPTH:DEPTH + Y, :], LANES - 1 - quarter - SPAN * i) * (1.0 / 9.0)
         ghost = ghost + pe[(p - DEPTH + 2) // 2, TOP:TOP + Y, :]
-        total = total + jnp.where(lane == 0, ghost, turn(mid, 1))
-        total = total + jnp.where(lane == LANES - 1, ghost, turn(mid, -1))
+        total = total + jnp.where(first, ghost, turn(mid, 1))
+        total = total + jnp.where(last, ghost, turn(mid, -1))
         return mid, 6.0 * mid - total
 
     load_x.wait()
-    lane = iota((Y, LANES), 1)
     out = jnp.zeros((Y, LANES), jnp.float32)
     for i in range(X):
         out = jnp.where(lane // 2 == i, turn(ux[1 + i, TOP:TOP + Y, :], 2 * i + 1), out)
@@ -498,15 +528,22 @@
     pl.semaphore_wait(barrier, n - 1)
     start_all(face_copies())
     load_b.wait()
+    for i in range(X):
+        mid, total = around(ux, 1 + i)
+        total = total + jnp.where(first, 0.0, turn(mid, 1))
+        total = total + jnp.where(last, 0.0, turn(mid, -1))
+        g0[0, DEPTH + i, TOP:TOP + Y, :] = bb[i] - (6.0 * mid - total)
     wait_all(face_copies())
+    for i, side in ((0, 1), (X - 1, 0)):
+        here = (0, DEPTH + i, slice(TOP, TOP + Y))
+        g0[here] = g0[here] + xg[side]
+    for j, side in ((0, 1), (Y - 1, 0)):
+        here = (0, slice(DEPTH, DEPTH + X), slice(TOP + j, TOP + j + 1))
+        g0[here] = g0[here] + yg[side]
     ghosts = jnp.where(lane % 2 == 0, turn(zi[1], -1), turn(zi[0], 1))
     for i in range(X):
-        mid, total = beside(ux, 1 + i, 1, TOP, Y)
-        mid, total = mid[0], total[0]
-        ghost = turn(ghosts, -2 * i - 1)
-        total = total + jnp.where(lane == 0, ghost, turn(mid, 1))
-        total = total + jnp.where(lane == LANES - 1, ghost, turn(mid, -1))
-        g0[0, DEPTH + i, TOP:TOP + Y, :] = bb[i] - (6.0 * mid - total)
+        here = (0, DEPTH + i, slice(TOP, TOP + Y))
+        g0[here] = g0[here] + jnp.where(first | last, turn(ghosts, -2 * i - 1), 0.0)
 
     def sums_of(a, b):
         return jnp.concatenate([jnp.sum(a, axis=0, keepdims=True), jnp.sum(b, axis=0, keepdims=True)], axis=0)
@@ -530,32 +567,27 @@
     for i in range(X):
         mid, image = operator(z1, DEPTH + i)
         here = (DEPTH + i, slice(TOP, TOP + Y))
-        zi0, w0 = z0[here], g0[(1,) + here]
-        r = g0[(0,) + here] - alpha * w0
-        zi1 = zi0 - alpha * mid
-        w1 = w0 - alpha * image
-        rz = rz + r * zi1
-        zw = zw + zi1 * w1
-        sol_ref[i] = ux[1 + i, TOP:TOP + Y, :] + alpha * zi0
+        before, w = z0[here], g0[(1,) + here]
+        r = g0[(0,) + here] - alpha * w
+        z = before - alpha * mid
+        w = w - alpha * image
+        rz = rz + r * z
+        zw = zw + z * w
+        sol_ref[i] = ux[1 + i, TOP:TOP + Y, :] + alpha * before
+        z_ref[i] = z
         res_ref[i] = r
-        bb[i] = zi1
-        wv[i] = w1
+        w_ref[i] = w
     sums = sums_of(rz, zw)
     ds[...] = sums
     dr[me] = sums
     to_all(ds, dr, dsend.at[0], drecv.at[0])
     sent_all(face_copies())
+    sent_around()
     for k in range(STEPS):
-        sent_all(z_copies(k))
-        sent_all(main_copies(k))
-        sent_more(k)
         all_done(cr.at[k], csend.at[k])
+    all_done(dr, dsend.at[0])
     all_done(dr, drecv.at[0])
-    alpha = ratio(dr[...])
-    for i in range(X):
-        sol_ref[i] = sol_ref[i] + alpha * bb[i]
-        res_ref[i] = res_ref[i] - alpha * wv[i]
-    all_done(dr, dsend.at[0])
+    alpha_ref[...] = jnp.broadcast_to(ratio(dr[...]), alpha_ref.shape)
 
 
 def solution(mesh):
@@ -578,30 +610,32 @@
         scratch = [
             vm(X + 2, Y + 2 * TOP, LANES), vm(*block),
             *(vm(STEPS, *e) for e in ext), vm(STEPS, *slab),
-            *(vm(*e) for e in ext for _ in range(2)), vm(*slab), vm(*slab),
-            vm(*ext[0]), vm(*ext[0]), vm(*block),
+            *(vm(*e) for e in ext + [slab] for _ in range(SWEEPS - 1)),
+            vm(*ext[0]), vm(*ext[0]),
             vm(slab[0], *tall[0]), vm(slab[0], *tall[0]),
             vm(dims[1][0] + 2, 2 * tall[1][0], LANES), vm(dims[1][0] + 2, 2 * tall[1][0], LANES),
             *(vm(*t) for t in tall), vm(*tall[0]),
             vm(cx * sizes[0] + DEPTH, cy * sizes[1], LANES),
             vm(cx + DEPTH, 2 * cy * sizes[1] + 2 * DEPTH, LANES),
             vm(X // 2, Y, LANES), vm(X // 2, 2 * Y, LANES),
-            vm(Y, LANES), vm(2, Y, LANES),
+            vm(2, Y, LANES), vm(2, X, 1, LANES), vm(Y, LANES), vm(2, Y, LANES),
             vm(STEPS, 2, zrows, LANES), vm(STEPS, 2, zrows, LANES),
             vm(STEPS, packed, 1, LANES), vm(STEPS, n, packed, 1, LANES),
-            vm(2, LANES), vm(n, 2, LANES),
-            dma(2), dma(6), dma(6), dma(STEPS, 2), dma(STEPS, 2),
-            dma(STEPS, 8), dma(STEPS, 8), dma(STEPS, HALOED, 8), dma(STEPS, HALOED, 8),
+            vm(2, LANES), vm(n, 2, LANES), vm(3 * STEPS * DEPTH * max(X, Y), LANES),
+            dma(2), dma(6), dma(6), dma(2), dma(STEPS, 2),
+            dma(8), dma(STEPS, 8), dma(STEPS, 8),
             dma(STEPS), dma(STEPS), dma(1), dma(1),
         ]
-        return tuple(pl.pallas_call(
+        whole = pltpu.VMEM(block, f32)
+        base, z, r, w, alpha = pl.pallas_call(
             functools.partial(kernel, sizes, block),
-            out_shape=(pltpu.VMEM(block, f32), pltpu.VMEM(block, f32)),
+            out_shape=(whole, whole, whole, whole, pltpu.VMEM((8, LANES), f32)),
             in_specs=[pl.BlockSpec(memory_space=pl.ANY)] * 2,
-            out_specs=[pl.BlockSpec(memory_space=pltpu.VMEM)] * 2,
+            out_specs=[pl.BlockSpec(memory_space=pltpu.VMEM)] * 5,
             scratch_shapes=scratch,
             compiler_params=pltpu.CompilerParams(collective_id=0, has_side_effects=True),
-        )(right_side, guess))
+        )(right_side, guess)
+        return base + alpha[0, 0] * z, r - alpha[0, 0] * w
 
     spec = P(*AXES)
     return jax.shard_map(run, mesh=mesh, in_specs=(spec, spec), out_specs=(spec, spec), check_vma=False)

time: 42 us -> 38.2 us (0.910)
  Pallas kernels: 39.6 us -> 35.1 us
  other arithmetic: 0 us -> 1.83 us
  local copies, waits for them, and re-layouts: 1.59 us -> 0.54 us
    pallas_call x1, Pallas kernels: 39.6 us -> 35.1 us  [run(): pl.pallas_call(functools.partial(kernel, sizes, block), out_shape=(whole,...]
    sub x0 -> x1, other arithmetic: none -> 1.83 us  [run(): return (base + alpha[0, 0] * z, r - alpha[0, 0] * w)]
    unnamed x2 -> x0, local copies, waits for them, and re-layouts: 1.59 us -> none
    slice x0 -> x1, local copies, waits for them, and re-layouts: none -> 0.54 us  [run(): return (base + alpha[0, 0] * z, r - alpha[0, 0] * w)]
where the time goes in v2:
time: 38.2 us; the launch traced here: 38.1 us
  Pallas kernels  35.1 us (92%)
  other arithmetic  1.83 us (5%)
  between operations  0.64 us (2%)
  local copies, waits for them, and re-layouts  0.54 us (1%)
    pallas_call x1, Pallas kernels, run(): pl.pallas_call(functools.partial(kernel, sizes, block), out_shape=(whole,...  35.1 us
    sub x1, other arithmetic, run(): return (base + alpha[0, 0] * z, r - alpha[0, 0] * w)  1.83 us

profile of v2, /device:TPU:0, one launch (start us, length us, event | category | flops | bytes accessed | tf_op | source)
XLA Modules:
  0.0 38.1 jit_solution(13423063814240059988)
XLA Ops:
  0.6 35.1 %shard_map.41 = (f32[32,32,128]{2,1,0:T(8,128)S(1)}, f32[32,32,128]{2,1,0:T(8,128)S(1)}, f32[32,32,128]{2,1,0:T(8,128)S(1)}, f32[32,32,128]{2,1,0:T(8,128)S(1)}, f32[8,128]{1,0:T(8,128)S(1)}) custom-call(f32[32,32,128]{2,1,0:T(8,128)} %b_hbm.1, f32[32,32,128]{2,1,0:T(8,128)} %x_hbm.1), custom_call_target="tpu_custom_call" | custom-call | tf_op jit(solution)/shard_map/pallas_call | solution.py:630
  35.7 0.5 %slice.4 = f32[1,1]{1,0:T(1,128)} slice(f32[8,128]{1,0:T(8,128)S(1)} %get-tuple-element.8), slice={[0:1], [0:1]} | slice | bytes 8 | tf_op jit(solution)/shard_map/slice | solution.py:638
  36.3 1.8 %multiply_subtract_fusion = (f32[32,32,128]{2,1,0:T(8,128)}, f32[32,32,128]{2,1,0:T(8,128)}) fusion(f32[32,32,128]{2,1,0:T(8,128)S(1)} %get-tuple-element.10, f32[32,32,128]{2,1,0:T(8,128)S(1)} %get-tuple-element.11, f32[]{:T(128)} %bitcast, f32[32,32,128]{2,1,0:T(8,128)S(1)} %get-tuple-element.7, f32[32,32,128]{2,1,0:T(8,128)S(1)} %get-tuple-element.9), kind=kLoop, calls=%fused_computation | loop fusion | flops 524288 | bytes 3145732 | tf_op jit(solution)/shard_map/sub | solution.py:638

commit v3 on v2

--- a/solution.py
+++ b/solution.py
@@ -10,15 +10,17 @@
 LEVELS = 6
 SWEEPS = 4
 STEPS = 2
-HALOED = 3
+HALOED = 4
 AXES = ("gx", "gy", "gz")
 LANES = 128
 TOP = 8
 DEPTH = SWEEPS
 SPAN = 8 * DEPTH
 PER = LANES // SPAN
+PARTS = 4
 MESH = pl.DeviceIdType.MESH
 HIGH = lax.Precision.HIGHEST
+ROWS = 8
 AROUND = [(a, b) for a in (-1, 0, 1) for b in (-1, 0, 1) if (a, b) != (0, 0)]
 FACES = [(d, s) for d in range(3) for s in (-1, 1)]
 
@@ -27,32 +29,18 @@
     return lax.broadcasted_iota(jnp.int32, shape, dim)
 
 
-def lanes_dot(x, matrix):
-    first, second, _ = x.shape
-    if second % 8 == 0:
-        out = jnp.dot(x.reshape(first * second, LANES), matrix, precision=HIGH, preferred_element_type=jnp.float32)
-        return out.reshape(first, second, LANES)
-    planes = [jnp.dot(x[i], matrix, precision=HIGH, preferred_element_type=jnp.float32)[None] for i in range(first)]
-    return jnp.concatenate(planes, axis=0)
-
-
 def take(x, index):
-    index = jnp.broadcast_to(index[:1], x.shape[-2:])
-    if x.ndim == 2:
-        return jnp.take_along_axis(x, index, axis=1, mode="promise_in_bounds")
-    return jnp.stack([jnp.take_along_axis(x[i], index, axis=1, mode="promise_in_bounds") for i in range(x.shape[0])])
-
-
-def halve_matrix(width, start):
-    source, target = iota((LANES, LANES), 0), iota((LANES, LANES), 1) - start
-    keep = (target >= 0) & (target < width) & ((source == 2 * target) | (source == 2 * target + 1))
-    return jnp.where(keep, 0.125, 0.0)
-
-
-def double_matrix(width, start):
-    source, target = iota((LANES, LANES), 0) - start, iota((LANES, LANES), 1)
-    keep = (source >= 0) & (source < width) & ((target == 2 * source) | (target == 2 * source + 1))
-    return jnp.where(keep, 1.0, 0.0)
+    if x.ndim == 3:
+        return jnp.stack([take(x[i], index) for i in range(x.shape[0])])
+    rows = x.shape[0]
+    more = -rows % 8
+    if rows == 1:
+        x = jnp.broadcast_to(x, (8, LANES))
+    elif more:
+        x = jnp.concatenate([x, jnp.zeros((more, LANES), x.dtype)], axis=0)
+    index = jnp.broadcast_to(index[:1], x.shape)
+    out = jnp.take_along_axis(x, index, axis=1, mode="promise_in_bounds")
+    return out[:rows] if more else out
 
 
 def wrapped(lane):
@@ -64,28 +52,14 @@
     return take(x + turn(x, -1), 2 * (lane % width)) * 0.125
 
 
-def plane_groups(shape, width):
-    return max(1, LANES // width // shape[1])
-
-
-def own_group(shape, width):
-    group = iota(shape, 0) % plane_groups(shape, width) * shape[1] + iota(shape, 1)
-    return iota(shape, 2) // width == group
-
-
-def gather_matrix(width, start):
-    source, target = iota((LANES, LANES), 0) % width, iota((LANES, LANES), 1) - start
-    return jnp.where(source == target, 1.0, 0.0)
-
-
 def turn(x, shift):
     shift = shift % LANES
     return pltpu.roll(x, shift, x.ndim - 1) if shift else x
 
 
 def kernel(sizes, block, b_hbm, x_hbm, sol_ref, z_ref, res_ref, w_ref, alpha_ref, *rest):
-    (ux, bb, g0, g1, g2, gs, f0a, f0b, f0c, f1a, f1b, f1c, f2a, f2b, f2c, fsa, fsb, fsc, z0, z1, sc, sd, pd, pe,
-     m0, m1, m2, ms, wref, wide, fold, spread, xg, yg, ze, zi, zs, zr, cs, cr, ds, dr, blank,
+    (ux, bb, g0, g1, g2, g3, gs, f0a, f0b, f0c, f1a, f1b, f1c, f2a, f2b, f2c, f3a, f3b, f3c, fsa, fsb, fsc,
+     z0, z1, sc, sd, pd, pe, m0, m1, m2, m3, ms, pmat, wref, wide, fold, spread, xg, yg, ze, zi, zs, zr, cs, cr, ds, dr, blank,
      isem, xsend, xrecv, zsend, zrecv, send, mrecv, frecv, csend, crecv, dsend, drecv) = rest
     nx, ny, nz = sizes
     n = nx * ny * nz
@@ -93,9 +67,9 @@
     me = (at[0] * ny + at[1]) * nz + at[2]
     dims = [tuple(d >> l for d in block) for l in range(LEVELS)]
     X, Y, Z = block
-    fields = (g0, g1, g2)
-    after = ((f0a, f0b, f0c), (f1a, f1b, f1c), (f2a, f2b, f2c), (fsa, fsb, fsc))
-    masks = (m0, m1, m2)
+    fields = (g0, g1, g2, g3)
+    after = ((f0a, f0b, f0c), (f1a, f1b, f1c), (f2a, f2b, f2c), (f3a, f3b, f3c), (fsa, fsb, fsc))
+    masks = (m0, m1, m2, m3)
     groups = X // PER
     lower = [at[d] > 0 for d in range(3)]
     upper = [at[d] < sizes[d] - 1 for d in range(3)]
@@ -108,8 +82,18 @@
     load_b.start()
 
     def others():
-        moved = [[lax.rem(at[d] + k, sizes[d]) if k else at[d] for k in range(sizes[d])] for d in range(3)]
-        return [(a, b, c) for a in moved[0] for b in moved[1] for c in moved[2]][1:]
+        out = []
+        for b in range(ny - 1, -1, -1):
+            for c in range(nz - 1, -1, -1):
+                for a in range(nx):
+                    if b or c:
+                        first = jnp.where(at[0] < nx // 2, nx - 1 - a, a)
+                    elif a:
+                        first = lax.rem(at[0] + a, nx)
+                    else:
+                        continue
+                    out.append((first, lax.rem(at[1] + b, ny), lax.rem(at[2] + c, nz)))
+        return out
 
     barrier = pltpu.get_barrier_semaphore()
     for target in others():
@@ -155,6 +139,16 @@
     for l in range(HALOED):
         lane = iota((dims[l][1] + 2 * DEPTH, LANES), 1)
         masks[l][...] = mask(dims[l][1], lane if l == 0 else wrapped(lane), dims[l][2])
+    CA, CB, CC = dims[HALOED]
+    CD = dims[HALOED + 1][2]
+    cells = CA * CB
+    row, column = iota(pmat.shape, 0), iota(pmat.shape, 1)
+    cell, device = column // n, column % n
+    plane, line = row // ROWS, row % ROWS
+    dx, dy = device // (ny * nz), device // nz % ny
+    fits = (cell < cells) & (plane == dx * CA + cell // CB) & (line == dy * CB + cell % CB)
+    fits = fits | ((cell == cells) & (plane == nx * CA + dx) & (line == dy))
+    pmat[...] = jnp.where(fits, 1.0, 0.0)
     lane = iota((Y + 2 * DEPTH, LANES), 1) % SPAN
     ms[...] = mask(Y, jnp.where(lane < SPAN // 2, lane + Z - SPAN // 4, lane - 3 * SPAN // 4), Z)
 
@@ -342,17 +336,17 @@
             scale = m * inlow[0] if g == 0 else m * inup[0] if g == groups + 1 else m
             dst[g, low:low + rows, :] = rhs[g, low:low + rows, :] + (3.0 * mid + total) * scale
 
-    def smooth_whole(rhs, width, l):
+    def smooth_whole(rhs, depth_y, depth_z, l):
         A, B, _ = rhs.shape
-        lane = iota(rhs.shape, 2)
+        lane, row = iota(rhs.shape, 2), iota(rhs.shape, 1)
         e = rhs
         for _ in range(SWEEPS - 1):
             px, py = jnp.zeros((1, B, LANES), jnp.float32), jnp.zeros((A, 1, LANES), jnp.float32)
             total = jnp.concatenate([px, e[:-1]], axis=0) + jnp.concatenate([e[1:], px], axis=0)
             total = total + jnp.concatenate([py, e[:, :-1]], axis=1) + jnp.concatenate([e[:, 1:], py], axis=1)
             total = total + jnp.where(lane == 0, 0.0, turn(e, 1))
-            total = total + jnp.where(lane == width - 1, 0.0, turn(e, -1))
-            e = rhs + (3.0 * e + total) * (1.0 / 9.0)
+            total = total + jnp.where(lane == depth_z - 1, 0.0, turn(e, -1))
+            e = rhs + jnp.where(row < depth_y, (3.0 * e + total) * (1.0 / 9.0), 0.0)
         return e * (4.0 ** l / 9.0)
 
     half, quarter = SPAN // 2, SPAN // 4
@@ -403,38 +397,37 @@
             fields[l][k, DEPTH + i, TOP:TOP + B, :] = jnp.where(
                 lane >= LANES - DEPTH, turn(below, -DEPTH - DEPTH * (A + i)), held)
 
-    width = dims[HALOED][2]
-    cx, cy, _ = dims[HALOED]
-    starts = [0, Y, Y + dims[1][1]]
-    packed = cx // plane_groups((cx, cy), width)
+    half_row = LANES // 2
+    starts = [sum(dims[i][1] for i in range(l)) for l in range(HALOED)]
+
+    def own_row(k):
+        lane = iota((1, LANES), 1)
+        out, total = jnp.zeros((1, LANES), jnp.float32), None
+        for i in range(CA):
+            for j in range(CB):
+                part = None
+                for a in (0, 1):
+                    for b in (0, 1):
+                        y = TOP + 2 * j + b
+                        one = fields[HALOED - 1][k, DEPTH + 2 * i + a, y:y + 1, :]
+                        part = one if part is None else part + one
+                part = halve(part, CC)
+                out = jnp.where(lane // CC == i * CB + j, part, out)
+                total = part if total is None else total + part
+        return jnp.where((lane >= cells * CC) & (lane < cells * CC + CD), halve(total, CD), out)
 
     def coarse(k):
-        per = plane_groups((cx, cy), width)
-        fine = None
-        for c in range(nz):
-            rows = []
-            for i in range(nx):
-                columns = []
-                for j in range(ny):
-                    part = cr[k, (i * ny + j) * nz + c, 0:packed][:, None]
-                    part = jnp.broadcast_to(part, (cx // per, per, cy, LANES)).reshape(cx, cy, LANES)
-                    columns.append(jnp.where(own_group((cx, cy, LANES), width), part, 0.0))
-                rows.append(jnp.concatenate(columns, axis=1))
-            spot = lanes_dot(jnp.concatenate(rows, axis=0), gather_matrix(width, c * width))
-            fine = spot if fine is None else fine + spot
-        chain = [fine]
-        widths = [width * nz]
-        for l in range(HALOED + 1, LEVELS):
-            widths.append(widths[-1] // 2)
-            chain.append(jnp.where(iota((1, 1, LANES), 2) < widths[-1], halve(fold_xy(chain[-1]), LANES // 2), 0.0))
-        whole = smooth_whole(chain[-1], widths[-1], LEVELS - 1)
-        for l in range(LEVELS - 2, HALOED - 1, -1):
-            i = l - HALOED
-            spread_y(whole, spread)
-            grown = spread[0:whole.shape[0], 0:2 * whole.shape[1], :]
-            grown = twice(take(grown, iota((8, LANES), 1) // 2))
-            whole = grown + smooth_whole(chain[i], widths[i], l)
-        wref[DEPTH // 2:DEPTH // 2 + nx * cx, :, :] = whole
+        rows = cr[k, :, 0, :]
+        lane, row = iota((n, LANES), 1), iota((n, LANES), 0)
+        parts = [jnp.where(lane // CC == row % nz, take(rows, cell * CC + lane % CC), 0.0) for cell in range(cells)]
+        parts.append(jnp.where(lane // CD == row % nz, take(rows, cells * CC + lane % CD), 0.0))
+        out = jnp.dot(pmat[...], jnp.concatenate(parts, axis=0), precision=HIGH, preferred_element_type=jnp.float32)
+        out = out.reshape(-1, ROWS, LANES)
+        last = smooth_whole(out[nx * CA:], ny, nz * CD, HALOED + 1)
+        spread_y(last, spread)
+        grown = take(spread[0:nx, 0:ROWS, :], iota((8, LANES), 1) // 2)
+        whole = twice(grown) + smooth_whole(out[:nx * CA], ny * CB, nz * CC, HALOED)
+        wref[DEPTH // 2:DEPTH // 2 + nx * CA, :, :] = whole
 
     def precondition(k, z, extra):
         start_all(main_copies(k))
@@ -446,11 +439,7 @@
             pack_level(k, l + 1, starts[l + 1])
         pack_slab(k)
         start_all(z_copies(k))
-        mine = halve(fold_xy(own(fields[HALOED - 1], HALOED - 1, k)), width)
-        mine = jnp.where(own_group(mine.shape, width), mine, 0.0)
-        mine = jnp.sum(mine.reshape(-1, plane_groups(mine.shape, width), *mine.shape[1:]), axis=1)
-        mine = jnp.sum(mine, axis=1, keepdims=True)
-        mine = jnp.concatenate([mine, extra], axis=0)
+        mine = own_row(k) if extra is None else jnp.where(iota((1, LANES), 1) < half_row, own_row(k), extra)
         cs[k] = mine
         cr[k, me] = mine
         to_all(cs.at[k], cr.at[k], csend.at[k], crecv.at[k])
@@ -466,16 +455,19 @@
             sweep_rim(after[0][s - 2] if s > 1 else g0.at[k], g0.at[k], after[0][s - 1], s)
         all_done(cr.at[k], crecv.at[k])
         coarse(k)
-        spread_y(wref[pl.ds(at[0] * cx, cx + DEPTH)], wide, DEPTH)
-        part = wide[:, pl.ds(pl.multiple_of(at[1] * 2 * cy, 8), 2 * cy + 2 * DEPTH), :]
-        source = (wrapped(lane) >> 1) + at[2] * width
-        inside = (source >= 0) & (source < width * nz)
+        A, B, C = dims[HALOED - 1]
+        spread_y(wref[pl.ds(at[0] * CA, CA + DEPTH)], wide, DEPTH)
+        part = wide[:, 0:2 * ROWS, :]
+        for j in range(1, ny):
+            part = jnp.where(at[1] == j, wide[:, j * B:j * B + 2 * ROWS, :], part)
+        source = (wrapped(lane) >> 1) + at[2] * CC
+        inside = (source >= 0) & (source < CC * nz)
         part = take(part, jnp.where(inside, source, 0))
         part = jnp.where(inside[0:1][None], part, 0.0)
-        part = twice(part)[DEPTH - 1:DEPTH + dims[HALOED - 1][0] + 1]
+        part = twice(part)[DEPTH - 1:DEPTH + A + 1, 0:B + 2 * DEPTH]
         wait_more(k)
         for s in range(1, SWEEPS):
-            sweep_slab(after[3][s - 2] if s > 1 else gs.at[k], gs.at[k], after[3][s - 1])
+            sweep_slab(after[HALOED][s - 2] if s > 1 else gs.at[k], gs.at[k], after[HALOED][s - 1])
             for l in range(1, HALOED):
                 sweep(l, after[l][s - 2] if s > 1 else fields[l].at[k], fields[l].at[k], after[l][s - 1], s)
         for l in range(HALOED - 1, 0, -1):
@@ -489,7 +481,7 @@
                 spread_y(take(full, lane // 2), pd)
                 spread_y(take(full, jnp.where(lane == 0, LANES - 1, C)), pe)
         low, rows = TOP - DEPTH, Y + 2 * DEPTH
-        slab = after[3][SWEEPS - 2]
+        slab = after[HALOED][SWEEPS - 2]
         spot = iota((rows, LANES), 1) % SPAN
         for g in range(groups + 2):
             s = slab[g, low:low + rows, :]
@@ -546,23 +538,29 @@
         g0[here] = g0[here] + jnp.where(first | last, turn(ghosts, -2 * i - 1), 0.0)
 
     def sums_of(a, b):
-        return jnp.concatenate([jnp.sum(a, axis=0, keepdims=True), jnp.sum(b, axis=0, keepdims=True)], axis=0)
-
-    def ratio(parts):
-        both = jnp.sum(parts, axis=0)
-        both = jnp.sum(both, axis=1, keepdims=True)
-        return both[0:1] / both[1:2]
+        lane = iota((1, LANES), 1)
+        pair = jnp.concatenate([jnp.sum(a, axis=0, keepdims=True), jnp.sum(b, axis=0, keepdims=True)], axis=0)
+        pair = pair + turn(pair, LANES // 2)
+        pair = pair + turn(pair, LANES // 4)
+        return jnp.where(lane < 3 * LANES // 4, pair[0:1], pair[1:2])
+
+    def ratio(rows):
+        lane = iota((1, LANES), 1)
+        row = jnp.sum(rows, axis=0, keepdims=True)
+        upper_half = jnp.where(lane >= 3 * LANES // 4, row, 0.0)
+        lower_half = jnp.where((lane >= half_row) & (lane < 3 * LANES // 4), row, 0.0)
+        return jnp.sum(lower_half, axis=1, keepdims=True) / jnp.sum(upper_half, axis=1, keepdims=True)
 
     nothing = jnp.zeros((Y, LANES), jnp.float32)
-    precondition(0, z0, jnp.zeros((2, 1, LANES), jnp.float32))
+    precondition(0, z0, None)
     rz, zw = nothing, nothing
     for i in range(X):
         mid, image = operator(z0, DEPTH + i)
         g0[1, DEPTH + i, TOP:TOP + Y, :] = image
         rz = rz + g0[0, DEPTH + i, TOP:TOP + Y, :] * mid
         zw = zw + mid * image
-    precondition(1, z1, sums_of(rz, zw)[:, None, :])
-    alpha = ratio(cr[1, :, packed:packed + 2, 0, :])
+    precondition(1, z1, sums_of(rz, zw))
+    alpha = ratio(cr[1, :, 0, :])
     rz, zw = nothing, nothing
     for i in range(X):
         mid, image = operator(z1, DEPTH + i)
@@ -587,7 +585,23 @@
         all_done(cr.at[k], csend.at[k])
     all_done(dr, dsend.at[0])
     all_done(dr, drecv.at[0])
-    alpha_ref[...] = jnp.broadcast_to(ratio(dr[...]), alpha_ref.shape)
+    alpha_ref[...] = jnp.broadcast_to(ratio(dr[:, 0, :]), alpha_ref.shape)
+
+
+def finish(base, z, r, w, alpha, sol, res, sol_out, res_out, sem):
+    X = base.shape[0]
+    size = X // PARTS
+    a = alpha[0:1, 0:1][None]
+    copies = []
+    for part in range(PARTS):
+        here = slice(part * size, (part + 1) * size)
+        sol_out[here] = base[here] + a * z[here]
+        res_out[here] = r[here] - a * w[here]
+        for i, (src, dst) in enumerate(((sol_out, sol), (res_out, res))):
+            copies.append(pltpu.make_async_copy(src.at[here], dst.at[here], sem.at[i, part]))
+            copies[-1].start()
+    for copy in copies:
+        copy.wait()
 
 
 def solution(mesh):
@@ -603,8 +617,8 @@
         ext = [(dims[l][0] + 2 * DEPTH, dims[l][1] + 2 * TOP, LANES) for l in range(HALOED)]
         slab = (X // PER + 2, Y + 2 * TOP, LANES)
         tall = [(dims[l][1] + 2 * DEPTH, LANES) for l in range(HALOED)]
-        cx, cy, width = dims[HALOED]
-        packed = cx // plane_groups((cx, cy), width) + 2
+        CA, CB, CC = dims[HALOED]
+        assert dims[HALOED + 1][:2] == (1, 1) and sizes[1] * CB <= ROWS and CA * CB * CC + CC // 2 <= LANES // 2
         zrows = sum(dims[l][1] for l in range(HALOED))
         dma = lambda *s: pltpu.SemaphoreType.DMA(s)
         scratch = [
@@ -615,13 +629,14 @@
             vm(slab[0], *tall[0]), vm(slab[0], *tall[0]),
             vm(dims[1][0] + 2, 2 * tall[1][0], LANES), vm(dims[1][0] + 2, 2 * tall[1][0], LANES),
             *(vm(*t) for t in tall), vm(*tall[0]),
-            vm(cx * sizes[0] + DEPTH, cy * sizes[1], LANES),
-            vm(cx + DEPTH, 2 * cy * sizes[1] + 2 * DEPTH, LANES),
+            vm((CA + 1) * sizes[0] * ROWS, (CA * CB + 1) * n),
+            vm(CA * sizes[0] + DEPTH, ROWS, LANES),
+            vm(CA + DEPTH, 4 * ROWS, LANES),
             vm(X // 2, Y, LANES), vm(X // 2, 2 * Y, LANES),
             vm(2, Y, LANES), vm(2, X, 1, LANES), vm(Y, LANES), vm(2, Y, LANES),
             vm(STEPS, 2, zrows, LANES), vm(STEPS, 2, zrows, LANES),
-            vm(STEPS, packed, 1, LANES), vm(STEPS, n, packed, 1, LANES),
-            vm(2, LANES), vm(n, 2, LANES), vm(3 * STEPS * DEPTH * max(X, Y), LANES),
+            vm(STEPS, 1, LANES), vm(STEPS, n, 1, LANES),
+            vm(1, LANES), vm(n, 1, LANES), vm(3 * STEPS * DEPTH * max(X, Y), LANES),
             dma(2), dma(6), dma(6), dma(2), dma(STEPS, 2),
             dma(8), dma(STEPS, 8), dma(STEPS, 8),
             dma(STEPS), dma(STEPS), dma(1), dma(1),
@@ -635,7 +650,15 @@
             scratch_shapes=scratch,
             compiler_params=pltpu.CompilerParams(collective_id=0, has_side_effects=True),
         )(right_side, guess)
-        return base + alpha[0, 0] * z, r - alpha[0, 0] * w
+        inner = [pltpu.with_memory_space_constraint(v, pltpu.VMEM) for v in (base, z, r, w, alpha)]
+        out = jax.ShapeDtypeStruct(block, f32)
+        return tuple(pl.pallas_call(
+            finish,
+            out_shape=(out, out),
+            in_specs=[pl.BlockSpec(memory_space=pltpu.VMEM)] * 5,
+            out_specs=[pl.BlockSpec(memory_space=pl.ANY)] * 2,
+            scratch_shapes=[vm(*block), vm(*block), dma(2, PARTS)],
+        )(*inner))
 
     spec = P(*AXES)
     return jax.shard_map(run, mesh=mesh, in_specs=(spec, spec), out_specs=(spec, spec), check_vma=False)

time: 38.2 us -> 37.4 us (0.979)
  other arithmetic: 1.83 us -> 0 us
  Pallas kernels: 35.1 us -> 36.6 us
  local copies, waits for them, and re-layouts: 0.54 us -> 0 us
    sub x1 -> x0, other arithmetic: 1.83 us -> none  [run(): return (base + alpha[0, 0] * z, r - alpha[0, 0] * w)]
    pallas_call x0 -> x1, Pallas kernels: none -> 1.08 us  [run(): pl.pallas_call(finish, out_shape=(out, out), in_specs=[pl.BlockSpec(memor...]
    slice x1 -> x0, local copies, waits for them, and re-layouts: 0.54 us -> none  [run(): return (base + alpha[0, 0] * z, r - alpha[0, 0] * w)]
    pallas_call x1, Pallas kernels: 35.1 us -> 35.6 us  [run(): pl.pallas_call(functools.partial(kernel, sizes, block), out_shape=(whole,...]
where the time goes in v3:
time: 37.4 us; the launch traced here: 37.3 us
  Pallas kernels  36.6 us (98%)
  between operations  0.64 us (2%)
    pallas_call x1, Pallas kernels, run(): pl.pallas_call(functools.partial(kernel, sizes, block), out_shape=(whole,...  35.6 us
    pallas_call x1, Pallas kernels, run(): pl.pallas_call(finish, out_shape=(out, out), in_specs=[pl.BlockSpec(memor...  1.08 us

profile of v3, /device:TPU:0, one launch (start us, length us, event | category | flops | bytes accessed | tf_op | source)
XLA Modules:
  0.0 37.3 jit_solution(5481214596127416898)
XLA Ops:
  0.6 35.6 %shard_map.41 = (f32[32,32,128]{2,1,0:T(8,128)S(1)}, f32[32,32,128]{2,1,0:T(8,128)S(1)}, f32[32,32,128]{2,1,0:T(8,128)S(1)}, f32[32,32,128]{2,1,0:T(8,128)S(1)}, f32[8,128]{1,0:T(8,128)S(1)}) custom-call(f32[32,32,128]{2,1,0:T(8,128)} %b_hbm.1, f32[32,32,128]{2,1,0:T(8,128)} %x_hbm.1), custom_call_target="tpu_custom_call" | custom-call | tf_op jit(solution)/shard_map/pallas_call | solution.py:645
  36.2 1.1 %shard_map.42 = (f32[32,32,128]{2,1,0:T(8,128)}, f32[32,32,128]{2,1,0:T(8,128)}) custom-call(f32[32,32,128]{2,1,0:T(8,128)S(1)} %get-tuple-element.7.base, f32[32,32,128]{2,1,0:T(8,128)S(1)} %get-tuple-element.8.z, f32[32,32,128]{2,1,0:T(8,128)S(1)} %get-tuple-element.9.r, f32[32,32,128]{2,1,0:T(8,128)S(1)} %get-tuple-element.10.w, ...), custom_call_target="tpu_custom_call" | custom-call | tf_op jit(solution)/shard_map/pallas_call | solution.py:655

commit v4 on v3

--- a/solution.py
+++ b/solution.py
@@ -21,6 +21,7 @@
 MESH = pl.DeviceIdType.MESH
 HIGH = lax.Precision.HIGHEST
 ROWS = 8
+ALL = [(a, b, c) for c in (-1, 1, 0) for a in (0, -1, 1) for b in (0, -1, 1) if (a, b, c) != (0, 0, 0)]
 AROUND = [(a, b) for a in (-1, 0, 1) for b in (-1, 0, 1) if (a, b) != (0, 0)]
 FACES = [(d, s) for d in range(3) for s in (-1, 1)]
 
@@ -58,9 +59,9 @@
 
 
 def kernel(sizes, block, b_hbm, x_hbm, sol_ref, z_ref, res_ref, w_ref, alpha_ref, *rest):
-    (ux, bb, g0, g1, g2, g3, gs, f0a, f0b, f0c, f1a, f1b, f1c, f2a, f2b, f2c, f3a, f3b, f3c, fsa, fsb, fsc,
-     z0, z1, sc, sd, pd, pe, m0, m1, m2, m3, ms, pmat, wref, wide, fold, spread, xg, yg, ze, zi, zs, zr, cs, cr, ds, dr, blank,
-     isem, xsend, xrecv, zsend, zrecv, send, mrecv, frecv, csend, crecv, dsend, drecv) = rest
+    (ux, bb, g0, g1, g2, g3, gs, h1, h2, h3, hs, f0a, f0b, f0c, f1a, f1b, f1c, f2a, f2b, f2c, f3a, f3b, f3c, fsa, fsb, fsc,
+     z0, z1, sc, sd, pd, pe, m0, m1, m2, m3, ms, pmat, wref, wide, fold, spread, xg, yg, ze, zi, zq0, zq1, zq2, zr0, zr1, zr2, es, zx, xs, xf, cs, cr, ds, dr, blank,
+     isem, xsend, xrecv, fsend, frecv, send, mrecv, csend, crecv, dsend, drecv) = rest
     nx, ny, nz = sizes
     n = nx * ny * nz
     at = tuple(lax.axis_index(a) for a in AXES)
@@ -70,6 +71,7 @@
     fields = (g0, g1, g2, g3)
     after = ((f0a, f0b, f0c), (f1a, f1b, f1c), (f2a, f2b, f2c), (f3a, f3b, f3c), (fsa, fsb, fsc))
     masks = (m0, m1, m2, m3)
+    whole = (None, h1, h2, h3, hs)
     groups = X // PER
     lower = [at[d] > 0 for d in range(3)]
     upper = [at[d] < sizes[d] - 1 for d in range(3)]
@@ -111,18 +113,29 @@
                     a = TOP + B if side else TOP - DEPTH
                     ref[k, :, a:a + DEPTH, :] = jnp.zeros((A + 2 * d, DEPTH, LANES), jnp.float32)
 
+    far = (zr0, zr1, zr2, zx, xf)
+
+    def nothing_in(ref):
+        ref[...] = jnp.zeros(ref.shape, jnp.float32)
+
     for side in (0, 1):
         for dim in range(2):
             @pl.when(jnp.logical_not((upper if side else lower)[dim]))
             def _(dim=dim, side=side):
                 outside(dim, side)
-                ref = (xg, yg)[dim]
-                ref[1 - side] = jnp.zeros(ref.shape[1:], jnp.float32)
+                nothing_in((xg, yg)[dim].at[1 - side])
+                for ref in far if dim else ():
+                    head = (slice(None),) * (len(ref.shape) - 2)
+                    a = ref.shape[-2] - DEPTH if side else 0
+                    nothing_in(ref.at[head + (slice(a, a + DEPTH),)])
+                if dim == 0:
+                    nothing_in(zx.at[:, :, side])
+                    nothing_in(xf.at[:, side])
         @pl.when(jnp.logical_not((upper if side else lower)[2]))
         def _(side=side):
-            zi[1 if side else 0] = jnp.zeros(zi.shape[1:], jnp.float32)
-            for k in range(STEPS):
-                zr[k, 0 if side else 1] = jnp.zeros(zr.shape[2:], jnp.float32)
+            nothing_in(zi.at[side])
+            for ref in far[:4]:
+                nothing_in(ref.at[:, 1 - side])
 
     ux[:, TOP - 1:TOP, :] = jnp.zeros((X + 2, 1, LANES), jnp.float32)
     ux[:, TOP + Y:TOP + Y + 1, :] = jnp.zeros((X + 2, 1, LANES), jnp.float32)
@@ -172,16 +185,6 @@
             out.append((copy, upper[d] if s > 0 else lower[d], lower[d] if s > 0 else upper[d]))
         return out
 
-    def z_copies(k):
-        out = []
-        for side in (0, 1):
-            copy = pltpu.make_async_remote_copy(
-                src_ref=zs.at[k, side], dst_ref=zr.at[k, side], send_sem=zsend.at[side], recv_sem=zrecv.at[k, side],
-                device_id=(at[0], at[1], at[2] + (1 if side else -1)), device_id_type=MESH,
-            )
-            out.append((copy, upper[2] if side else lower[2], lower[2] if side else upper[2]))
-        return out
-
     def span(step, depth, start, own, other):
         if step > 0:
             return (start + own - depth, depth), (start - depth, depth)
@@ -211,11 +214,52 @@
     def main_copies(k):
         return around_copies(g0, k, DEPTH, X, Y, mrecv)
 
-    def more_copies(k):
-        out = [around_copies(gs, k, 1, groups, Y, frecv)]
-        for l in range(1, HALOED):
-            out.append(around_copies(fields[l], k, DEPTH, dims[l][0], dims[l][1], frecv))
-        return [[kind[i] for kind in out] for i in range(len(AROUND))]
+    def rows_of(dy, rows):
+        if dy > 0:
+            return pl.ds(rows - DEPTH, DEPTH), pl.ds(0, DEPTH), DEPTH
+        if dy < 0:
+            return pl.ds(0, DEPTH), pl.ds(rows + DEPTH, DEPTH), DEPTH
+        return pl.ds(0, rows), pl.ds(DEPTH, rows), rows
+
+    def every(conds):
+        out = None
+        for cond in conds:
+            out = cond if out is None else jnp.logical_and(out, cond)
+        return out
+
+    def far_copies(k):
+        out = []
+        for i, (dx, dy, dz) in enumerate(ALL):
+            step = (dx, dy, dz)
+            to = every([(upper if t > 0 else lower)[d] for d, t in enumerate(step) if t])
+            fro = every([(lower if t > 0 else upper)[d] for d, t in enumerate(step) if t])
+            from_x, into_x = (1, 0) if dx > 0 else (0, 1)
+            side = 1 if dz > 0 else 0
+            pairs = []
+            if dz and dx:
+                a, b, c = rows_of(dy, Y)
+                pairs.append((es.at[k, from_x, a], zx.at[k, side, into_x, b], c))
+            elif dz:
+                for src, dst in ((zq0.at[k, side], zr0), (zq1.at[k], zr1), (zq2.at[k], zr2)):
+                    a, b, c = rows_of(dy, src.shape[0])
+                    pairs.append((src.at[a], dst.at[k, side, b], c))
+            else:
+                arrays = [(gs, 1, groups, Y)]
+                if dx:
+                    a, b, c = rows_of(dy, dims[1][1])
+                    pairs.append((xs.at[k, from_x, :, a], xf.at[k, into_x, :, b], DEPTH * c))
+                else:
+                    arrays += [(fields[l], DEPTH, dims[l][0], dims[l][1]) for l in range(1, HALOED)]
+                for ref, depth, planes, rows in arrays:
+                    (sx, lx), (tx, _) = span(dx, depth, depth, planes, None)
+                    (sy, ly), (ty, _) = span(dy, DEPTH, TOP, rows, None)
+                    pairs.append((ref.at[k, sx:sx + lx, sy:sy + ly], ref.at[k, tx:tx + lx, ty:ty + ly], lx * ly))
+            copies = [pltpu.make_async_remote_copy(
+                src_ref=src, dst_ref=dst, send_sem=fsend.at[i], recv_sem=frecv.at[k, i],
+                device_id=(at[0] + dx, at[1] + dy, at[2] + dz), device_id_type=MESH,
+            ) for src, dst, _ in pairs]
+            out.append((copies, to, fro, sum(c for _, _, c in pairs)))
+        return out
 
     def lines(copies):
         return sum(entry[3] for entry in copies)
@@ -236,25 +280,22 @@
         for copy, cond, *_ in copies:
             pl.when(cond)(copy.wait_send)
 
-    def start_more(k):
-        for same in more_copies(k):
-            @pl.when(same[0][1])
-            def _(same=same):
-                for copy, *_ in same:
+    def start_far(k):
+        for copies, to, _, _ in far_copies(k):
+            @pl.when(to)
+            def _(copies=copies):
+                for copy in copies:
                     copy.start()
 
-    def wait_more(k):
-        for i, same in enumerate(more_copies(k)):
-            pl.when(same[0][2])(lambda i=i, same=same: bytes_done(lines(same), frecv.at[k, i]))
+    def wait_far(k):
+        for i, (_, _, fro, count) in enumerate(far_copies(k)):
+            pl.when(fro)(lambda i=i, count=count: bytes_done(count, frecv.at[k, i]))
 
     def sent_around():
-        for i, same in enumerate(more_copies(0)):
-            count = STEPS * (lines(same) + lines([main_copies(0)[i]]))
-            pl.when(same[0][1])(lambda i=i, count=count: bytes_done(count, send.at[i]))
-        for side in (0, 1):
-            part = zs.at[:, side]
-            cond = upper[2] if side else lower[2]
-            pl.when(cond)(pltpu.make_async_copy(part, part, zsend.at[side]).wait)
+        for i, (_, to, _, count) in enumerate(far_copies(0)):
+            pl.when(to)(lambda i=i, count=count: bytes_done(STEPS * count, fsend.at[i]))
+        for i, entry in enumerate(main_copies(0)):
+            pl.when(entry[1])(lambda i=i, entry=entry: bytes_done(STEPS * entry[3], send.at[i]))
 
     def to_all(src, dst, s_sem, r_sem):
         for target in others():
@@ -365,41 +406,101 @@
             here = spot // DEPTH == g
             low = jnp.where(here, turn(both, DEPTH * g - quarter), low)
             high = jnp.where(here, turn(both, DEPTH * g - quarter + DEPTH), high)
-        zs[k, 0, 0:Y, :] = low
-        zs[k, 1, 0:Y, :] = high
-
-    def pack_level(k, l, first):
+        zq0[k, 0] = low
+        zq0[k, 1] = high
+        for side, j in ((0, 0), (1, groups - 1)):
+            es[k, side] = put(0, low, j, 0) + put(0, high, j, 1)
+
+    def slots(l):
+        return (0, 0, 0, dims[2][0] // DEPTH * 2)[l], dims[l][0] // DEPTH
+
+    def put(l, x, source, target):
+        lane = iota(x.shape, 1)
+        return jnp.where(lane % SPAN // DEPTH == target, turn(x, DEPTH * (target - source)), 0.0)
+
+    def pack_level(k, l):
         A, B, C = dims[l]
+        base, many = slots(l)
         lane = iota((B, LANES), 1)
+        line, slot = lane // SPAN, lane % SPAN // DEPTH
         out = jnp.zeros((B, LANES), jnp.float32)
         for i in range(A):
             field = fields[l][k, DEPTH + i, TOP:TOP + B, :]
-            out = jnp.where(lane // DEPTH == i, turn(field, DEPTH * i), out)
-            out = jnp.where(lane // DEPTH == A + i, turn(field, DEPTH * (A + i) - C + DEPTH), out)
+            x, j = i % DEPTH, i // DEPTH
+            lo, hi = base + j, base + many + j
+            out = jnp.where((line == x) & (slot == lo), turn(field, SPAN * x + DEPTH * lo), out)
+            out = jnp.where((line == x) & (slot == hi), turn(field, SPAN * x + DEPTH * hi - C + DEPTH), out)
+        return out
+
+    def pack_rest(k):
+        one, two, three = [pack_level(k, l) for l in range(1, HALOED)]
+        zq1[k] = one
+        B1, B2, B3 = [dims[l][1] for l in range(1, HALOED)]
+        zq2[k, 0:B2] = two
+        for a in (0, B2 - B3):
+            zq2[k, a:a + B3] = zq2[k, a:a + B3] + three
         for side in (0, 1):
-            zs[k, side, first:first + B, :] = out
+            def edge(l, x):
+                base, many = slots(l)
+                j = many - 1 if side else 0
+                return put(l, x, base + j, 2 * l) + put(l, x, base + many + j, 2 * l + 1)
+            first, second, third = edge(1, one), edge(2, two), edge(3, three)
+            for src, dst, size, part in (
+                    (0, 0, B1 - DEPTH, first), (B1 - DEPTH, Y - DEPTH, DEPTH, first),
+                    (0, 0, DEPTH, second), (B2 - DEPTH, Y - DEPTH, DEPTH, second),
+                    (0, 0, DEPTH, third), (0, Y - DEPTH, DEPTH, third)):
+                es[k, side, dst:dst + size] = es[k, side, dst:dst + size] + part[src:src + size]
+            for x in range(DEPTH):
+                p1, p2, p3 = [DEPTH + x + (dims[l][0] - DEPTH if side else 0) for l in range(1, HALOED)]
+                xs[k, side, x] = g1[k, p1, TOP:TOP + B1, :]
+                second = turn(g2[k, p2, TOP:TOP + B2, :], dims[1][2])
+                third = turn(g3[k, p3, TOP:TOP + B3, :], dims[1][2] + dims[2][2])
+                xs[k, side, x, 0:DEPTH] = xs[k, side, x, 0:DEPTH] + second[0:DEPTH] + third
+                xs[k, side, x, B1 - DEPTH:B1] = xs[k, side, x, B1 - DEPTH:B1] + second[B2 - DEPTH:B2] + third
 
     def unpack_slab(k):
-        spot = iota((Y, LANES), 1) % SPAN
-        above, below = zr[k, 0, 0:Y, :], zr[k, 1, 0:Y, :]
-        for g in range(groups):
-            held = gs[k, g + 1, TOP:TOP + Y, :]
-            held = jnp.where(spot // DEPTH == 2, turn(above, 2 * DEPTH - DEPTH * g), held)
-            gs[k, g + 1, TOP:TOP + Y, :] = jnp.where(spot // DEPTH == 5, turn(below, 5 * DEPTH - DEPTH * g), held)
-
-    def unpack_level(k, l, first):
+        low, rows = TOP - DEPTH, Y + 2 * DEPTH
+        spot = iota((rows, LANES), 1) % SPAN
+        for g in range(groups + 2):
+            edge = 0 if g == 0 else 1 if g == groups + 1 else None
+            if edge is None:
+                above, below, up, down = zr0[k, 0], zr0[k, 1], g - 1, g - 1
+            else:
+                above, below, up, down = zx[k, 0, edge], zx[k, 1, edge], 0, 1
+            held = gs[k, g, low:low + rows, :]
+            held = jnp.where(spot // DEPTH == 2, turn(above, DEPTH * (2 - up)), held)
+            hs[g, low:low + rows, :] = jnp.where(spot // DEPTH == 5, turn(below, DEPTH * (5 - down)), held)
+
+    def unpack_level(k, l):
         A, B, C = dims[l]
-        lane = iota((B, LANES), 1)
-        above, below = zr[k, 0, first:first + B, :], zr[k, 1, first:first + B, :]
-        for i in range(A):
-            held = fields[l][k, DEPTH + i, TOP:TOP + B, :]
-            held = jnp.where(lane // DEPTH == C // DEPTH, turn(above, C - DEPTH * i), held)
-            fields[l][k, DEPTH + i, TOP:TOP + B, :] = jnp.where(
-                lane >= LANES - DEPTH, turn(below, -DEPTH - DEPTH * (A + i)), held)
+        low, rows = TOP - DEPTH, B + 2 * DEPTH
+        base, many = slots(l)
+        lane = iota((rows, LANES), 1)
+
+        def cut(ref, head):
+            end = ref.shape[-2]
+            tail = 0 if end == rows else (2 * DEPTH if B > DEPTH else DEPTH)
+            a = ref[head + (slice(0, rows - tail),)]
+            return jnp.concatenate([a, ref[head + (slice(end - tail, end),)]], axis=0) if tail else a
+
+        ref = (None, zr1, zr2, zr2)[l]
+        sides = [cut(ref, (k, 0)), cut(ref, (k, 1))]
+        edges = [[cut(zx, (k, side, e)) for side in (0, 1)] for e in (0, 1)]
+        start = sum(dims[i][2] for i in range(1, l))
+        for p in range(A + 2 * DEPTH):
+            edge = 0 if p < DEPTH else 1 if p >= DEPTH + A else None
+            x, j = p % DEPTH, p // DEPTH - 1
+            if edge is None:
+                held = fields[l][k, p, low:low + rows, :]
+                (above, below), up, down = sides, base + j, base + many + j
+            else:
+                held = jnp.where(lane < C, turn(cut(xf, (k, edge, x)), -start), 0.0)
+                (above, below), up, down = edges[edge], 2 * l, 2 * l + 1
+            held = jnp.where(lane // DEPTH == C // DEPTH, turn(above, C - SPAN * x - DEPTH * up), held)
+            whole[l][p, low:low + rows, :] = jnp.where(
+                lane >= LANES - DEPTH, turn(below, -DEPTH - SPAN * x - DEPTH * down), held)
 
     half_row = LANES // 2
-    starts = [sum(dims[i][1] for i in range(l)) for l in range(HALOED)]
-
     def own_row(k):
         lane = iota((1, LANES), 1)
         out, total = jnp.zeros((1, LANES), jnp.float32), None
@@ -426,8 +527,8 @@
         last = smooth_whole(out[nx * CA:], ny, nz * CD, HALOED + 1)
         spread_y(last, spread)
         grown = take(spread[0:nx, 0:ROWS, :], iota((8, LANES), 1) // 2)
-        whole = twice(grown) + smooth_whole(out[:nx * CA], ny * CB, nz * CC, HALOED)
-        wref[DEPTH // 2:DEPTH // 2 + nx * CA, :, :] = whole
+        wref[DEPTH // 2:DEPTH // 2 + nx * CA, :, :] = (
+            twice(grown) + smooth_whole(out[:nx * CA], ny * CB, nz * CC, HALOED))
 
     def precondition(k, z, extra):
         start_all(main_copies(k))
@@ -436,23 +537,26 @@
             A, B, C = dims[l + 1]
             coarser = jnp.where(iota((1, 1, LANES), 2) < C, halve(fold_xy(own(fields[l], l, k)), LANES // 2), 0.0)
             fields[l + 1][k, DEPTH:DEPTH + A, TOP:TOP + B, :] = coarser
-            pack_level(k, l + 1, starts[l + 1])
         pack_slab(k)
-        start_all(z_copies(k))
+        pack_rest(k)
+        start_far(k)
         mine = own_row(k) if extra is None else jnp.where(iota((1, LANES), 1) < half_row, own_row(k), extra)
         cs[k] = mine
         cr[k, me] = mine
         to_all(cs.at[k], cr.at[k], csend.at[k], crecv.at[k])
         for s in range(1, SWEEPS):
             sweep_inside(after[0][s - 2] if s > 1 else g0.at[k], g0.at[k], after[0][s - 1], s)
-        wait_all(z_copies(k))
-        unpack_slab(k)
-        for l in range(1, HALOED):
-            unpack_level(k, l, starts[l])
-        start_more(k)
         wait_all(main_copies(k))
         for s in range(1, SWEEPS):
             sweep_rim(after[0][s - 2] if s > 1 else g0.at[k], g0.at[k], after[0][s - 1], s)
+        wait_far(k)
+        unpack_slab(k)
+        for l in range(1, HALOED):
+            unpack_level(k, l)
+        for s in range(1, SWEEPS):
+            sweep_slab(after[HALOED][s - 2] if s > 1 else hs, hs, after[HALOED][s - 1])
+            for l in range(1, HALOED):
+                sweep(l, after[l][s - 2] if s > 1 else whole[l], whole[l], after[l][s - 1], s)
         all_done(cr.at[k], crecv.at[k])
         coarse(k)
         A, B, C = dims[HALOED - 1]
@@ -465,11 +569,6 @@
         part = take(part, jnp.where(inside, source, 0))
         part = jnp.where(inside[0:1][None], part, 0.0)
         part = twice(part)[DEPTH - 1:DEPTH + A + 1, 0:B + 2 * DEPTH]
-        wait_more(k)
-        for s in range(1, SWEEPS):
-            sweep_slab(after[HALOED][s - 2] if s > 1 else gs.at[k], gs.at[k], after[HALOED][s - 1])
-            for l in range(1, HALOED):
-                sweep(l, after[l][s - 2] if s > 1 else fields[l].at[k], fields[l].at[k], after[l][s - 1], s)
         for l in range(HALOED - 1, 0, -1):
             A, B, C = dims[l]
             end = after[l][SWEEPS - 2][DEPTH - 1:DEPTH + A + 1, TOP - DEPTH:TOP + B + DEPTH, :]
@@ -619,11 +718,11 @@
         tall = [(dims[l][1] + 2 * DEPTH, LANES) for l in range(HALOED)]
         CA, CB, CC = dims[HALOED]
         assert dims[HALOED + 1][:2] == (1, 1) and sizes[1] * CB <= ROWS and CA * CB * CC + CC // 2 <= LANES // 2
-        zrows = sum(dims[l][1] for l in range(HALOED))
         dma = lambda *s: pltpu.SemaphoreType.DMA(s)
         scratch = [
             vm(X + 2, Y + 2 * TOP, LANES), vm(*block),
             *(vm(STEPS, *e) for e in ext), vm(STEPS, *slab),
+            *(vm(*e) for e in ext[1:]), vm(*slab),
             *(vm(*e) for e in ext + [slab] for _ in range(SWEEPS - 1)),
             vm(*ext[0]), vm(*ext[0]),
             vm(slab[0], *tall[0]), vm(slab[0], *tall[0]),
@@ -634,11 +733,14 @@
             vm(CA + DEPTH, 4 * ROWS, LANES),
             vm(X // 2, Y, LANES), vm(X // 2, 2 * Y, LANES),
             vm(2, Y, LANES), vm(2, X, 1, LANES), vm(Y, LANES), vm(2, Y, LANES),
-            vm(STEPS, 2, zrows, LANES), vm(STEPS, 2, zrows, LANES),
+            vm(STEPS, 2, Y, LANES), vm(STEPS, dims[1][1], LANES), vm(STEPS, dims[2][1], LANES),
+            *(vm(STEPS, 2, dims[l][1] + 2 * DEPTH, LANES) for l in range(HALOED - 1)),
+            vm(STEPS, 2, Y, LANES), vm(STEPS, 2, 2, Y + 2 * DEPTH, LANES),
+            vm(STEPS, 2, DEPTH, dims[1][1], LANES), vm(STEPS, 2, DEPTH, dims[1][1] + 2 * DEPTH, LANES),
             vm(STEPS, 1, LANES), vm(STEPS, n, 1, LANES),
             vm(1, LANES), vm(n, 1, LANES), vm(3 * STEPS * DEPTH * max(X, Y), LANES),
-            dma(2), dma(6), dma(6), dma(2), dma(STEPS, 2),
-            dma(8), dma(STEPS, 8), dma(STEPS, 8),
+            dma(2), dma(6), dma(6), dma(len(ALL)), dma(STEPS, len(ALL)),
+            dma(8), dma(STEPS, 8),
             dma(STEPS), dma(STEPS), dma(1), dma(1),
         ]
         whole = pltpu.VMEM(block, f32)

time: 37.4 us -> 34.9 us (0.933)
  Pallas kernels: 36.6 us -> 34.1 us
    pallas_call x1, Pallas kernels: 35.6 us -> 33 us  [run(): pl.pallas_call(functools.partial(kernel, sizes, block), out_shape=(whole,...]
where the time goes in v4:
time: 34.9 us; the launch traced here: 34.7 us
  Pallas kernels  34.1 us (98%)
  between operations  0.64 us (2%)
    pallas_call x1, Pallas kernels, run(): pl.pallas_call(functools.partial(kernel, sizes, block), out_shape=(whole,...  33 us
    pallas_call x1, Pallas kernels, run(): pl.pallas_call(finish, out_shape=(out, out), in_specs=[pl.BlockSpec(memor...  1.08 us

profile of v4, /device:TPU:0, one launch (start us, length us, event | category | flops | bytes accessed | tf_op | source)
XLA Modules:
  0.0 34.7 jit_solution(15025262342740776022)
XLA Ops:
  0.6 33.0 %shard_map.41 = (f32[32,32,128]{2,1,0:T(8,128)S(1)}, f32[32,32,128]{2,1,0:T(8,128)S(1)}, f32[32,32,128]{2,1,0:T(8,128)S(1)}, f32[32,32,128]{2,1,0:T(8,128)S(1)}, f32[8,128]{1,0:T(8,128)S(1)}) custom-call(f32[32,32,128]{2,1,0:T(8,128)} %b_hbm.1, f32[32,32,128]{2,1,0:T(8,128)} %x_hbm.1), custom_call_target="tpu_custom_call" | custom-call | tf_op jit(solution)/shard_map/pallas_call | solution.py:747
  33.7 1.1 %shard_map.42 = (f32[32,32,128]{2,1,0:T(8,128)}, f32[32,32,128]{2,1,0:T(8,128)}) custom-call(f32[32,32,128]{2,1,0:T(8,128)S(1)} %get-tuple-element.7.base, f32[32,32,128]{2,1,0:T(8,128)S(1)} %get-tuple-element.8.z, f32[32,32,128]{2,1,0:T(8,128)S(1)} %get-tuple-element.9.r, f32[32,32,128]{2,1,0:T(8,128)S(1)} %get-tuple-element.10.w, ...), custom_call_target="tpu_custom_call" | custom-call | tf_op jit(solution)/shard_map/pallas_call | solution.py:757

commit v5 on v4

--- a/solution.py
+++ b/solution.py
@@ -61,7 +61,7 @@
 def kernel(sizes, block, b_hbm, x_hbm, sol_ref, z_ref, res_ref, w_ref, alpha_ref, *rest):
     (ux, bb, g0, g1, g2, g3, gs, h1, h2, h3, hs, f0a, f0b, f0c, f1a, f1b, f1c, f2a, f2b, f2c, f3a, f3b, f3c, fsa, fsb, fsc,
      z0, z1, sc, sd, pd, pe, m0, m1, m2, m3, ms, pmat, wref, wide, fold, spread, xg, yg, ze, zi, zq0, zq1, zq2, zr0, zr1, zr2, es, zx, xs, xf, cs, cr, ds, dr, blank,
-     isem, xsend, xrecv, fsend, frecv, send, mrecv, csend, crecv, dsend, drecv) = rest
+     isem, xsend, xrecv, frecv, send, mrecv, csend, crecv, dsend, drecv) = rest
     nx, ny, nz = sizes
     n = nx * ny * nz
     at = tuple(lax.axis_index(a) for a in AXES)
@@ -179,7 +179,7 @@
             else:
                 src, dst = ze, zi.at[0 if s > 0 else 1]
             copy = pltpu.make_async_remote_copy(
-                src_ref=src, dst_ref=dst, send_sem=xsend.at[i], recv_sem=xrecv.at[i],
+                src_ref=src, dst_ref=dst, send_sem=xsend.at[0], recv_sem=xrecv.at[0],
                 device_id=tuple(target), device_id_type=MESH,
             )
             out.append((copy, upper[d] if s > 0 else lower[d], lower[d] if s > 0 else upper[d]))
@@ -199,7 +199,7 @@
             (sy, ly), (ty, _) = span(dy, DEPTH, TOP, rows, None)
             copy = pltpu.make_async_remote_copy(
                 src_ref=ref.at[k, sx:sx + lx, sy:sy + ly], dst_ref=ref.at[k, tx:tx + lx, ty:ty + ly],
-                send_sem=send.at[i], recv_sem=rsem.at[k, i],
+                send_sem=send.at[0], recv_sem=rsem.at[k],
                 device_id=(at[0] + dx, at[1] + dy, at[2]), device_id_type=MESH,
             )
             to, fro = None, None
@@ -255,30 +255,45 @@
                     (sy, ly), (ty, _) = span(dy, DEPTH, TOP, rows, None)
                     pairs.append((ref.at[k, sx:sx + lx, sy:sy + ly], ref.at[k, tx:tx + lx, ty:ty + ly], lx * ly))
             copies = [pltpu.make_async_remote_copy(
-                src_ref=src, dst_ref=dst, send_sem=fsend.at[i], recv_sem=frecv.at[k, i],
+                src_ref=src, dst_ref=dst, send_sem=send.at[0], recv_sem=frecv.at[k],
                 device_id=(at[0] + dx, at[1] + dy, at[2] + dz), device_id_type=MESH,
             ) for src, dst, _ in pairs]
             out.append((copies, to, fro, sum(c for _, _, c in pairs)))
         return out
 
-    def lines(copies):
-        return sum(entry[3] for entry in copies)
-
     def bytes_done(count, sem):
+        assert count <= blank.shape[0]
         part = blank.at[pl.ds(0, count)]
         pltpu.make_async_copy(part, part, sem).wait()
+
+    def all_of(entries, sem, sign):
+        def nest(d, have):
+            if d == len(sizes):
+                total = sum(c for step, c in entries if all(t == 0 or sign * t in have[i] for i, t in enumerate(step)))
+                if total:
+                    bytes_done(total, sem)
+            elif sizes[d] == 1 or not any(step[d] for step, _ in entries):
+                nest(d + 1, have + [()])
+            else:
+                pl.when(jnp.logical_not(lower[d]))(lambda: nest(d + 1, have + [(1,)]))
+                pl.when(jnp.logical_not(upper[d]))(lambda: nest(d + 1, have + [(-1,)]))
+                if sizes[d] > 2:
+                    pl.when(jnp.logical_and(lower[d], upper[d]))(lambda: nest(d + 1, have + [(-1, 1)]))
+
+        nest(0, [])
+
+    def main_entries():
+        return [((dx, dy, 0), entry[3]) for (dx, dy), entry in zip(AROUND, main_copies(0))]
+
+    def far_entries():
+        return [(step, entry[3]) for step, entry in zip(ALL, far_copies(0))]
+
+    def face_entries():
+        return [(tuple(s if i == d else 0 for i in range(3)), X if d == 1 else Y) for d, s in FACES]
 
     def start_all(copies):
         for copy, cond, *_ in copies:
             pl.when(cond)(copy.start)
-
-    def wait_all(copies):
-        for copy, _, cond, *_ in copies:
-            pl.when(cond)(copy.wait_recv)
-
-    def sent_all(copies):
-        for copy, cond, *_ in copies:
-            pl.when(cond)(copy.wait_send)
 
     def start_far(k):
         for copies, to, _, _ in far_copies(k):
@@ -286,16 +301,6 @@
             def _(copies=copies):
                 for copy in copies:
                     copy.start()
-
-    def wait_far(k):
-        for i, (_, _, fro, count) in enumerate(far_copies(k)):
-            pl.when(fro)(lambda i=i, count=count: bytes_done(count, frecv.at[k, i]))
-
-    def sent_around():
-        for i, (_, to, _, count) in enumerate(far_copies(0)):
-            pl.when(to)(lambda i=i, count=count: bytes_done(STEPS * count, fsend.at[i]))
-        for i, entry in enumerate(main_copies(0)):
-            pl.when(entry[1])(lambda i=i, entry=entry: bytes_done(STEPS * entry[3], send.at[i]))
 
     def to_all(src, dst, s_sem, r_sem):
         for target in others():
@@ -533,23 +538,26 @@
     def precondition(k, z, extra):
         start_all(main_copies(k))
         lane = iota((8, LANES), 1)
-        for l in range(HALOED - 1):
-            A, B, C = dims[l + 1]
-            coarser = jnp.where(iota((1, 1, LANES), 2) < C, halve(fold_xy(own(fields[l], l, k)), LANES // 2), 0.0)
-            fields[l + 1][k, DEPTH:DEPTH + A, TOP:TOP + B, :] = coarser
+        sums = own(g0, 0, k)
+        for l in range(1, HALOED):
+            A, B, C = dims[l]
+            sums = fold_xy(sums)
+            sums = sums + turn(sums, -(1 << (l - 1)))
+            coarser = jnp.where(lane[0:1][None] < C, take(sums, (1 << l) * (lane % C)) * 0.125 ** l, 0.0)
+            fields[l][k, DEPTH:DEPTH + A, TOP:TOP + B, :] = coarser
         pack_slab(k)
         pack_rest(k)
-        start_far(k)
         mine = own_row(k) if extra is None else jnp.where(iota((1, LANES), 1) < half_row, own_row(k), extra)
         cs[k] = mine
         cr[k, me] = mine
-        to_all(cs.at[k], cr.at[k], csend.at[k], crecv.at[k])
+        start_far(k)
+        to_all(cs.at[k], cr.at[k], csend.at[0], crecv.at[k])
         for s in range(1, SWEEPS):
             sweep_inside(after[0][s - 2] if s > 1 else g0.at[k], g0.at[k], after[0][s - 1], s)
-        wait_all(main_copies(k))
+        all_of(main_entries(), mrecv.at[k], -1)
         for s in range(1, SWEEPS):
             sweep_rim(after[0][s - 2] if s > 1 else g0.at[k], g0.at[k], after[0][s - 1], s)
-        wait_far(k)
+        all_of(far_entries(), frecv.at[k], -1)
         unpack_slab(k)
         for l in range(1, HALOED):
             unpack_level(k, l)
@@ -624,7 +632,7 @@
         total = total + jnp.where(first, 0.0, turn(mid, 1))
         total = total + jnp.where(last, 0.0, turn(mid, -1))
         g0[0, DEPTH + i, TOP:TOP + Y, :] = bb[i] - (6.0 * mid - total)
-    wait_all(face_copies())
+    all_of(face_entries(), xrecv.at[0], -1)
     for i, side in ((0, 1), (X - 1, 0)):
         here = (0, DEPTH + i, slice(TOP, TOP + Y))
         g0[here] = g0[here] + xg[side]
@@ -678,10 +686,10 @@
     ds[...] = sums
     dr[me] = sums
     to_all(ds, dr, dsend.at[0], drecv.at[0])
-    sent_all(face_copies())
-    sent_around()
-    for k in range(STEPS):
-        all_done(cr.at[k], csend.at[k])
+    all_of(face_entries(), xsend.at[0], 1)
+    all_of([(step, STEPS * c) for step, c in main_entries() + far_entries()], send.at[0], 1)
+    part = cr.at[:, pl.ds(0, n - 1)]
+    pltpu.make_async_copy(part, part, csend.at[0]).wait()
     all_done(dr, dsend.at[0])
     all_done(dr, drecv.at[0])
     alpha_ref[...] = jnp.broadcast_to(ratio(dr[:, 0, :]), alpha_ref.shape)
@@ -738,10 +746,9 @@
             vm(STEPS, 2, Y, LANES), vm(STEPS, 2, 2, Y + 2 * DEPTH, LANES),
             vm(STEPS, 2, DEPTH, dims[1][1], LANES), vm(STEPS, 2, DEPTH, dims[1][1] + 2 * DEPTH, LANES),
             vm(STEPS, 1, LANES), vm(STEPS, n, 1, LANES),
-            vm(1, LANES), vm(n, 1, LANES), vm(3 * STEPS * DEPTH * max(X, Y), LANES),
-            dma(2), dma(6), dma(6), dma(len(ALL)), dma(STEPS, len(ALL)),
-            dma(8), dma(STEPS, 8),
-            dma(STEPS), dma(STEPS), dma(1), dma(1),
+            vm(1, LANES), vm(n, 1, LANES), vm(16 * STEPS * DEPTH * max(X, Y), LANES),
+            dma(2), dma(1), dma(1), dma(STEPS), dma(1), dma(STEPS),
+            dma(1), dma(STEPS), dma(1), dma(1),
         ]
         whole = pltpu.VMEM(block, f32)
         base, z, r, w, alpha = pl.pallas_call(

time: 34.9 us -> 33.9 us (0.971)
  Pallas kernels: 34.1 us -> 33.2 us
    pallas_call x1, Pallas kernels: 33 us -> 32.1 us  [run(): pl.pallas_call(functools.partial(kernel, sizes, block), out_shape=(whole,...]
where the time goes in v5:
time: 33.9 us; the launch traced here: 33.8 us
  Pallas kernels  33.2 us (98%)
  between operations  0.64 us (2%)
    pallas_call x1, Pallas kernels, run(): pl.pallas_call(functools.partial(kernel, sizes, block), out_shape=(whole,...  32.1 us
    pallas_call x1, Pallas kernels, run(): pl.pallas_call(finish, out_shape=(out, out), in_specs=[pl.BlockSpec(memor...  1.08 us

profile of v5, /device:TPU:0, one launch (start us, length us, event | category | flops | bytes accessed | tf_op | source)
XLA Modules:
  0.0 33.8 jit_solution(7749698207944520729)
XLA Ops:
  0.6 32.1 %shard_map.41 = (f32[32,32,128]{2,1,0:T(8,128)S(1)}, f32[32,32,128]{2,1,0:T(8,128)S(1)}, f32[32,32,128]{2,1,0:T(8,128)S(1)}, f32[32,32,128]{2,1,0:T(8,128)S(1)}, f32[8,128]{1,0:T(8,128)S(1)}) custom-call(f32[32,32,128]{2,1,0:T(8,128)} %b_hbm.1, f32[32,32,128]{2,1,0:T(8,128)} %x_hbm.1), custom_call_target="tpu_custom_call" | custom-call | tf_op jit(solution)/shard_map/pallas_call | solution.py:754
  32.7 1.1 %shard_map.42 = (f32[32,32,128]{2,1,0:T(8,128)}, f32[32,32,128]{2,1,0:T(8,128)}) custom-call(f32[32,32,128]{2,1,0:T(8,128)S(1)} %get-tuple-element.7.base, f32[32,32,128]{2,1,0:T(8,128)S(1)} %get-tuple-element.8.z, f32[32,32,128]{2,1,0:T(8,128)S(1)} %get-tuple-element.9.r, f32[32,32,128]{2,1,0:T(8,128)S(1)} %get-tuple-element.10.w, ...), custom_call_target="tpu_custom_call" | custom-call | tf_op jit(solution)/shard_map/pallas_call | solution.py:764

commit v6 on v5

--- a/solution.py
+++ b/solution.py
@@ -244,11 +244,12 @@
                     a, b, c = rows_of(dy, src.shape[0])
                     pairs.append((src.at[a], dst.at[k, side, b], c))
             else:
-                arrays = [(gs, 1, groups, Y)]
+                arrays = []
                 if dx:
                     a, b, c = rows_of(dy, dims[1][1])
                     pairs.append((xs.at[k, from_x, :, a], xf.at[k, into_x, :, b], DEPTH * c))
                 else:
+                    arrays = [(gs, 1, groups, Y)]
                     arrays += [(fields[l], DEPTH, dims[l][0], dims[l][1]) for l in range(1, HALOED)]
                 for ref, depth, planes, rows in arrays:
                     (sx, lx), (tx, _) = span(dx, depth, depth, planes, None)
@@ -415,6 +416,18 @@
         zq0[k, 1] = high
         for side, j in ((0, 0), (1, groups - 1)):
             es[k, side] = put(0, low, j, 0) + put(0, high, j, 1)
+
+    def pack_ends(k):
+        low, rows = TOP - DEPTH, Y + 2 * DEPTH
+        lane = iota((rows, LANES), 1)
+        line, spot = lane // SPAN, lane % SPAN
+        for g, p in ((0, 0), (groups + 1, DEPTH + X)):
+            both = jnp.zeros((rows, LANES), jnp.float32)
+            for i in range(PER):
+                field = g0[k, p + i, low:low + rows, :]
+                both = jnp.where((line == i) & (spot < half), turn(field, SPAN * i + quarter), both)
+            gs[k, g, low:low + rows, :] = jnp.where(
+                spot < quarter, both, jnp.where(spot >= 3 * quarter, turn(both, half), 0.0))
 
     def slots(l):
         return (0, 0, 0, dims[2][0] // DEPTH * 2)[l], dims[l][0] // DEPTH
@@ -536,7 +549,7 @@
             twice(grown) + smooth_whole(out[:nx * CA], ny * CB, nz * CC, HALOED))
 
     def precondition(k, z, extra):
-        start_all(main_copies(k))
+        start_all([main_copies(k)[i] for i, (dx, _) in enumerate(AROUND) if not dx])
         lane = iota((8, LANES), 1)
         sums = own(g0, 0, k)
         for l in range(1, HALOED):
@@ -555,6 +568,7 @@
         for s in range(1, SWEEPS):
             sweep_inside(after[0][s - 2] if s > 1 else g0.at[k], g0.at[k], after[0][s - 1], s)
         all_of(main_entries(), mrecv.at[k], -1)
+        pack_ends(k)
         for s in range(1, SWEEPS):
             sweep_rim(after[0][s - 2] if s > 1 else g0.at[k], g0.at[k], after[0][s - 1], s)
         all_of(far_entries(), frecv.at[k], -1)
@@ -636,13 +650,23 @@
     for i, side in ((0, 1), (X - 1, 0)):
         here = (0, DEPTH + i, slice(TOP, TOP + Y))
         g0[here] = g0[here] + xg[side]
-    for j, side in ((0, 1), (Y - 1, 0)):
-        here = (0, slice(DEPTH, DEPTH + X), slice(TOP + j, TOP + j + 1))
-        g0[here] = g0[here] + yg[side]
     ghosts = jnp.where(lane % 2 == 0, turn(zi[1], -1), turn(zi[0], 1))
-    for i in range(X):
-        here = (0, DEPTH + i, slice(TOP, TOP + Y))
-        g0[here] = g0[here] + jnp.where(first | last, turn(ghosts, -2 * i - 1), 0.0)
+
+    def complete(a, b):
+        for j, side in ((0, 1), (Y - 1, 0)):
+            here = (0, slice(DEPTH + a, DEPTH + b), slice(TOP + j, TOP + j + 1))
+            g0[here] = g0[here] + yg[side, a:b]
+        for i in range(a, b):
+            here = (0, DEPTH + i, slice(TOP, TOP + Y))
+            g0[here] = g0[here] + jnp.where(first | last, turn(ghosts, -2 * i - 1), 0.0)
+
+    def start_edges(k):
+        start_all([main_copies(k)[i] for i, (dx, _) in enumerate(AROUND) if dx])
+
+    complete(0, DEPTH)
+    complete(X - DEPTH, X)
+    start_edges(0)
+    complete(DEPTH, X - DEPTH)
 
     def sums_of(a, b):
         lane = iota((1, LANES), 1)
@@ -661,7 +685,10 @@
     nothing = jnp.zeros((Y, LANES), jnp.float32)
     precondition(0, z0, None)
     rz, zw = nothing, nothing
-    for i in range(X):
+    inner = list(range(DEPTH, X - DEPTH))
+    for i in [i for i in range(X) if i not in inner] + inner:
+        if i == DEPTH:
+            start_edges(1)
         mid, image = operator(z0, DEPTH + i)
         g0[1, DEPTH + i, TOP:TOP + Y, :] = image
         rz = rz + g0[0, DEPTH + i, TOP:TOP + Y, :] * mid

time: 33.9 us -> 33.1 us (0.976)
  Pallas kernels: 33.2 us -> 32.3 us
    pallas_call x1, Pallas kernels: 32.1 us -> 31.2 us  [run(): pl.pallas_call(functools.partial(kernel, sizes, block), out_shape=(whole,...]
where the time goes in v6:
time: 33.1 us; the launch traced here: 32.9 us
  Pallas kernels  32.3 us (98%)
  between operations  0.64 us (2%)
    pallas_call x1, Pallas kernels, run(): pl.pallas_call(functools.partial(kernel, sizes, block), out_shape=(whole,...  31.2 us
    pallas_call x1, Pallas kernels, run(): pl.pallas_call(finish, out_shape=(out, out), in_specs=[pl.BlockSpec(memor...  1.08 us

profile of v6, /device:TPU:0, one launch (start us, length us, event | category | flops | bytes accessed | tf_op | source)
XLA Modules:
  0.0 32.9 jit_solution(17809713054086374941)
XLA Ops:
  0.6 31.2 %shard_map.41 = (f32[32,32,128]{2,1,0:T(8,128)S(1)}, f32[32,32,128]{2,1,0:T(8,128)S(1)}, f32[32,32,128]{2,1,0:T(8,128)S(1)}, f32[32,32,128]{2,1,0:T(8,128)S(1)}, f32[8,128]{1,0:T(8,128)S(1)}) custom-call(f32[32,32,128]{2,1,0:T(8,128)} %b_hbm.1, f32[32,32,128]{2,1,0:T(8,128)} %x_hbm.1), custom_call_target="tpu_custom_call" | custom-call | tf_op jit(solution)/shard_map/pallas_call | solution.py:781
  31.9 1.1 %shard_map.42 = (f32[32,32,128]{2,1,0:T(8,128)}, f32[32,32,128]{2,1,0:T(8,128)}) custom-call(f32[32,32,128]{2,1,0:T(8,128)S(1)} %get-tuple-element.7.base, f32[32,32,128]{2,1,0:T(8,128)S(1)} %get-tuple-element.8.z, f32[32,32,128]{2,1,0:T(8,128)S(1)} %get-tuple-element.9.r, f32[32,32,128]{2,1,0:T(8,128)S(1)} %get-tuple-element.10.w, ...), custom_call_target="tpu_custom_call" | custom-call | tf_op jit(solution)/shard_map/pallas_call | solution.py:791

commit v7 on v6

--- a/solution.py
+++ b/solution.py
@@ -668,19 +668,21 @@
     start_edges(0)
     complete(DEPTH, X - DEPTH)
 
-    def sums_of(a, b):
+    def sums_of(a, b, width):
         lane = iota((1, LANES), 1)
         pair = jnp.concatenate([jnp.sum(a, axis=0, keepdims=True), jnp.sum(b, axis=0, keepdims=True)], axis=0)
-        pair = pair + turn(pair, LANES // 2)
-        pair = pair + turn(pair, LANES // 4)
-        return jnp.where(lane < 3 * LANES // 4, pair[0:1], pair[1:2])
-
-    def ratio(rows):
+        size = LANES // 2
+        while size >= width:
+            pair = pair + turn(pair, size)
+            size //= 2
+        return jnp.where(lane < LANES - width, pair[0:1], pair[1:2])
+
+    def ratio(rows, width):
         lane = iota((1, LANES), 1)
         row = jnp.sum(rows, axis=0, keepdims=True)
-        upper_half = jnp.where(lane >= 3 * LANES // 4, row, 0.0)
-        lower_half = jnp.where((lane >= half_row) & (lane < 3 * LANES // 4), row, 0.0)
-        return jnp.sum(lower_half, axis=1, keepdims=True) / jnp.sum(upper_half, axis=1, keepdims=True)
+        second = jnp.where(lane >= LANES - width, row, 0.0)
+        first = jnp.where((lane >= LANES - 2 * width) & (lane < LANES - width), row, 0.0)
+        return jnp.sum(first, axis=1, keepdims=True) / jnp.sum(second, axis=1, keepdims=True)
 
     nothing = jnp.zeros((Y, LANES), jnp.float32)
     precondition(0, z0, None)
@@ -693,8 +695,8 @@
         g0[1, DEPTH + i, TOP:TOP + Y, :] = image
         rz = rz + g0[0, DEPTH + i, TOP:TOP + Y, :] * mid
         zw = zw + mid * image
-    precondition(1, z1, sums_of(rz, zw))
-    alpha = ratio(cr[1, :, 0, :])
+    precondition(1, z1, sums_of(rz, zw, LANES // 4))
+    alpha = ratio(cr[1, :, 0, :], LANES // 4)
     rz, zw = nothing, nothing
     for i in range(X):
         mid, image = operator(z1, DEPTH + i)
@@ -705,21 +707,24 @@
         w = w - alpha * image
         rz = rz + r * z
         zw = zw + z * w
-        sol_ref[i] = ux[1 + i, TOP:TOP + Y, :] + alpha * before
-        z_ref[i] = z
-        res_ref[i] = r
         w_ref[i] = w
-    sums = sums_of(rz, zw)
+    sums = sums_of(rz, zw, LANES // 2)
     ds[...] = sums
     dr[me] = sums
     to_all(ds, dr, dsend.at[0], drecv.at[0])
+    for i in range(X):
+        here = (DEPTH + i, slice(TOP, TOP + Y))
+        before = z0[here]
+        sol_ref[i] = ux[1 + i, TOP:TOP + Y, :] + alpha * before
+        z_ref[i] = before - alpha * z1[here]
+        res_ref[i] = g0[(0,) + here] - alpha * g0[(1,) + here]
     all_of(face_entries(), xsend.at[0], 1)
     all_of([(step, STEPS * c) for step, c in main_entries() + far_entries()], send.at[0], 1)
     part = cr.at[:, pl.ds(0, n - 1)]
     pltpu.make_async_copy(part, part, csend.at[0]).wait()
     all_done(dr, dsend.at[0])
     all_done(dr, drecv.at[0])
-    alpha_ref[...] = jnp.broadcast_to(ratio(dr[:, 0, :]), alpha_ref.shape)
+    alpha_ref[...] = jnp.broadcast_to(ratio(dr[:, 0, :], LANES // 2), alpha_ref.shape)
 
 
 def finish(base, z, r, w, alpha, sol, res, sol_out, res_out, sem):

time: 33.1 us -> 33.1 us (level)
  no operation moved by 1% of the time
where the time goes in v7:
time: 33.1 us; the launch traced here: 32.9 us
  Pallas kernels  32.3 us (98%)
  between operations  0.64 us (2%)
    pallas_call x1, Pallas kernels, run(): pl.pallas_call(functools.partial(kernel, sizes, block), out_shape=(whole,...  31.2 us
    pallas_call x1, Pallas kernels, run(): pl.pallas_call(finish, out_shape=(out, out), in_specs=[pl.BlockSpec(memor...  1.08 us

profile of v7, /device:TPU:0, one launch (start us, length us, event | category | flops | bytes accessed | tf_op | source)
XLA Modules:
  0.0 32.9 jit_solution(13849819822344767771)
XLA Ops:
  0.6 31.2 %shard_map.41 = (f32[32,32,128]{2,1,0:T(8,128)S(1)}, f32[32,32,128]{2,1,0:T(8,128)S(1)}, f32[32,32,128]{2,1,0:T(8,128)S(1)}, f32[32,32,128]{2,1,0:T(8,128)S(1)}, f32[8,128]{1,0:T(8,128)S(1)}) custom-call(f32[32,32,128]{2,1,0:T(8,128)} %b_hbm.1, f32[32,32,128]{2,1,0:T(8,128)} %x_hbm.1), custom_call_target="tpu_custom_call" | custom-call | tf_op jit(solution)/shard_map/pallas_call | solution.py:786
  31.8 1.1 %shard_map.42 = (f32[32,32,128]{2,1,0:T(8,128)}, f32[32,32,128]{2,1,0:T(8,128)}) custom-call(f32[32,32,128]{2,1,0:T(8,128)S(1)} %get-tuple-element.7.base, f32[32,32,128]{2,1,0:T(8,128)S(1)} %get-tuple-element.8.z, f32[32,32,128]{2,1,0:T(8,128)S(1)} %get-tuple-element.9.r, f32[32,32,128]{2,1,0:T(8,128)S(1)} %get-tuple-element.10.w, ...), custom_call_target="tpu_custom_call" | custom-call | tf_op jit(solution)/shard_map/pallas_call | solution.py:796

commit v8 on v7

--- a/solution.py
+++ b/solution.py
@@ -21,7 +21,7 @@
 MESH = pl.DeviceIdType.MESH
 HIGH = lax.Precision.HIGHEST
 ROWS = 8
-ALL = [(a, b, c) for c in (-1, 1, 0) for a in (0, -1, 1) for b in (0, -1, 1) if (a, b, c) != (0, 0, 0)]
+ALL = [(a, b, c) for a in (-1, 1, 0) for c in (0, -1, 1) for b in (0, -1, 1) if (a, b, c) != (0, 0, 0)]
 AROUND = [(a, b) for a in (-1, 0, 1) for b in (-1, 0, 1) if (a, b) != (0, 0)]
 FACES = [(d, s) for d in range(3) for s in (-1, 1)]
 

time: 33.1 us -> 34 us (1.027)
  Pallas kernels: 32.3 us -> 33.2 us
    pallas_call x1, Pallas kernels: 31.2 us -> 32.1 us  [run(): pl.pallas_call(functools.partial(kernel, sizes, block), out_shape=(whole,...]
where the time goes in v8:
time: 34 us; the launch traced here: 33.8 us
  Pallas kernels  33.2 us (98%)
  between operations  0.64 us (2%)
    pallas_call x1, Pallas kernels, run(): pl.pallas_call(functools.partial(kernel, sizes, block), out_shape=(whole,...  32.1 us
    pallas_call x1, Pallas kernels, run(): pl.pallas_call(finish, out_shape=(out, out), in_specs=[pl.BlockSpec(memor...  1.08 us

profile of v8, /device:TPU:0, one launch (start us, length us, event | category | flops | bytes accessed | tf_op | source)
XLA Modules:
  0.0 33.8 jit_solution(5534904063704520060)
XLA Ops:
  0.6 32.1 %shard_map.41 = (f32[32,32,128]{2,1,0:T(8,128)S(1)}, f32[32,32,128]{2,1,0:T(8,128)S(1)}, f32[32,32,128]{2,1,0:T(8,128)S(1)}, f32[32,32,128]{2,1,0:T(8,128)S(1)}, f32[8,128]{1,0:T(8,128)S(1)}) custom-call(f32[32,32,128]{2,1,0:T(8,128)} %b_hbm.1, f32[32,32,128]{2,1,0:T(8,128)} %x_hbm.1), custom_call_target="tpu_custom_call" | custom-call | tf_op jit(solution)/shard_map/pallas_call | solution.py:786
  32.7 1.1 %shard_map.42 = (f32[32,32,128]{2,1,0:T(8,128)}, f32[32,32,128]{2,1,0:T(8,128)}) custom-call(f32[32,32,128]{2,1,0:T(8,128)S(1)} %get-tuple-element.7.base, f32[32,32,128]{2,1,0:T(8,128)S(1)} %get-tuple-element.8.z, f32[32,32,128]{2,1,0:T(8,128)S(1)} %get-tuple-element.9.r, f32[32,32,128]{2,1,0:T(8,128)S(1)} %get-tuple-element.10.w, ...), custom_call_target="tpu_custom_call" | custom-call | tf_op jit(solution)/shard_map/pallas_call | solution.py:796
